TPU v7x, 32 devices: a 4x4x1 block of a 4x4x8 slice. The times are simulated.
32 devices in a mesh: batch: 1 (over z), gz: 4 (over y), gy: 4 (over x), gx: 2 (over core).
Axes of the slice: x: 4, y: 4, z: 1, core: 2. Of those that a mesh axis runs over, the one named last changes fastest.
The devices are a block of a 4x4x8 slice.
Arguments:
- u_init: float32 [64, 256, 256], P(('batch', 'gx'), 'gy', 'gz')
- f_rhs: float32 [64, 256, 256], P(('batch', 'gx'), 'gy', 'gz')
- kappa_cell: float32 [64, 256, 256], P(('batch', 'gx'), 'gy', 'gz')
- stencil_w: float32 [26], replicated
- omega_sweep: float32 [32], replicated
Outputs:
- output: float32 [64, 256, 256], P(('batch', 'gx'), 'gy', 'gz')
All inputs are finite; a program needn't handle non-finite values.
Results may differ from a plain program's by a relative error of at most 0.001.
Values are sent between devices in bfloat16 or wider.
A program may use at most 768 MiB of HBM per device.

v0:
```python
import jax
import jax.numpy as jnp
from jax import lax
from jax.sharding import PartitionSpec as P, NamedSharding

MESH_AXES = ("gx", "gy", "gz")


def offset_list():
    unit_steps = (-1, 0, 1)
    return [(a, b, c) for a in unit_steps for b in unit_steps for c in unit_steps if (a, b, c) != (0, 0, 0)]


def window(array_in, offset, out_shape):
    lo_x = 1 + offset[0]
    lo_y = 1 + offset[1]
    lo_z = 1 + offset[2]
    return array_in[..., lo_x:lo_x + out_shape[0], lo_y:lo_y + out_shape[1], lo_z:lo_z + out_shape[2]]


def diag_sum(kappa_ext, stencil_w, out_shape):
    k_mid = window(kappa_ext, (0, 0, 0), out_shape)
    diag_total = jnp.zeros_like(k_mid)
    for w_idx, offset in enumerate(offset_list()):
        diag_total = diag_total + stencil_w[w_idx] * (0.5 * (k_mid + window(kappa_ext, offset, out_shape)))
    return diag_total


def jacobi_step(u_ext, kappa_ext, f_reg, diag_reg, stencil_w, relax_now):
    out_shape = f_reg.shape[-3:]
    u_mid = window(u_ext, (0, 0, 0), out_shape)
    k_mid = window(kappa_ext, (0, 0, 0), out_shape)
    applied = jnp.zeros_like(u_mid)
    for w_idx, offset in enumerate(offset_list()):
        coef_io = stencil_w[w_idx] * (0.5 * (k_mid + window(kappa_ext, offset, out_shape)))
        applied = applied + coef_io * (u_mid - window(u_ext, offset, out_shape))
    return u_mid + relax_now * (f_reg - applied) / diag_reg


def halo_axis(brick_in, axis_name, axis_size, axis_dim, halo_depth):
    extent = brick_in.shape[axis_dim]
    low_part = lax.slice_in_dim(brick_in, 0, halo_depth, axis=axis_dim)
    high_part = lax.slice_in_dim(brick_in, extent - halo_depth, extent, axis=axis_dim)
    to_next = [(source_idx, (source_idx + 1) % axis_size) for source_idx in range(axis_size)]
    to_prev = [(source_idx, (source_idx - 1) % axis_size) for source_idx in range(axis_size)]
    from_prev = lax.ppermute(high_part, axis_name, to_next)
    from_next = lax.ppermute(low_part, axis_name, to_prev)
    return jnp.concatenate([from_prev, brick_in, from_next], axis=axis_dim)


def halo_all(brick_in, axis_sizes, halo_depth):
    padded = brick_in
    for axis_dim, axis_name in enumerate(MESH_AXES):
        padded = halo_axis(padded, axis_name, axis_sizes[axis_dim], axis_dim, halo_depth)
    return padded


def solution(mesh):
    axis_sizes = tuple(mesh.shape[axis_name] for axis_name in MESH_AXES)
    brick_spec = P(("batch", "gx"), "gy", "gz")

    def local_sweeps(u_brick, f_brick, kappa_brick, stencil_w, omega_sweep):
        kappa_ext = halo_all(kappa_brick, axis_sizes, 1)
        diag_brick = diag_sum(kappa_ext, stencil_w, f_brick.shape)

        def sweep_body(sweep_idx, u_now):
            u_ext = halo_all(u_now, axis_sizes, 1)
            return jacobi_step(u_ext, kappa_ext, f_brick, diag_brick, stencil_w, omega_sweep[sweep_idx])

        return lax.fori_loop(0, omega_sweep.shape[0], sweep_body, u_brick)

    return jax.shard_map(local_sweeps, mesh=mesh, in_specs=(brick_spec, brick_spec, brick_spec, P(), P()), out_specs=brick_spec, check_vma=False)
```

profile of v0, /device:TPU:97, one launch (start us, length us, event | category | flops | bytes accessed | tf_op | source)
XLA Modules:
  0.0 1327.8 jit_solution(6511248905370588134)
XLA Ops:
  36.9 3.2 maximum_maximum_fusion.1
  40.1 16.2 %multiply_add_fusion = (f32[32,64,64]{2,1,0:T(8,128)}, f32[32,64,64]{2,1,0:T(8,128)}, f32[32,64,64]{2,1,0:T(8,128)}, f32[32,64,64]{2,1,0:T(8,128)}, f32[32,64,64...) fusion(f32[]{:T(128)} %bitcast.26, f32[]{:T(128)} %bitcast.25, ...), kind=kLoop, calls=%fused_computation.146 | loop fusion | flops 11141120 | bytes 24724584 | tf_op jit(solution)/shard_map/add | solution.py:25
  56.3 1271.3 %while.15 = (s32[]{:T(128)}, f32[32,64,64]{2,1,0:T(8,128)}, f32[32]{0:T(128)}, f32[]{:T(128)}, f32[32,64,64]{2,1,0:T(8,128)}, /*index=5*/f32[]{:T(128)}, f32[32,...) while((s32[]{:T(128)}, f32[32,64,64]{2,1,0:T(8,128)}, ...), condition=%wide.region_1.0_spmd, body=%wide.region_0.0_spmd.sunk | while | flops 16235674 | bytes 34852724 | solution.py:70
  76.1 3.2 maximum_maximum_fusion.3
  79.3 17.3 %divide_add_fusion.2 = f32[32,64,64]{2,1,0:T(8,128)} fusion(f32[32,64,64]{2,1,0:T(8,128)S(1)} %copy.71, f32[32,64,64]{2,1,0:T(8,128)} %get-tuple-element.1253, f32[32,64,64]{2,1,0:T(8,128)} %get-tuple-element.1252, f32[34,66,65]{2,1,0:T(8,128)S(1)} %get-tuple-element.1079, f32[32,64,64]{2,1,0:T(8,128)} %get-tuple-element.1251, ...), kind=kLoop, calls=%fused_computation.97.clone.1 | loop fusion | flops 15073280 | bytes 25773164 | tf_op jit(solution)/shard_map/while/body/eval_jaxpr/add | solution.py:37
  115.8 3.2 maximum_maximum_fusion.3
  119.0 17.3 %divide_add_fusion.2 = f32[32,64,64]{2,1,0:T(8,128)} fusion(f32[32,64,64]{2,1,0:T(8,128)S(1)} %copy.71, f32[32,64,64]{2,1,0:T(8,128)} %get-tuple-element.1253, f32[32,64,64]{2,1,0:T(8,128)} %get-tuple-element.1252, f32[34,66,65]{2,1,0:T(8,128)S(1)} %get-tuple-element.1079, f32[32,64,64]{2,1,0:T(8,128)} %get-tuple-element.1251, ...), kind=kLoop, calls=%fused_computation.97.clone.1 | loop fusion | flops 15073280 | bytes 25773164 | tf_op jit(solution)/shard_map/while/body/eval_jaxpr/add | solution.py:37
  155.5 3.2 maximum_maximum_fusion.3
  158.7 17.3 %divide_add_fusion.2 = f32[32,64,64]{2,1,0:T(8,128)} fusion(f32[32,64,64]{2,1,0:T(8,128)S(1)} %copy.71, f32[32,64,64]{2,1,0:T(8,128)} %get-tuple-element.1253, f32[32,64,64]{2,1,0:T(8,128)} %get-tuple-element.1252, f32[34,66,65]{2,1,0:T(8,128)S(1)} %get-tuple-element.1079, f32[32,64,64]{2,1,0:T(8,128)} %get-tuple-element.1251, ...), kind=kLoop, calls=%fused_computation.97.clone.1 | loop fusion | flops 15073280 | bytes 25773164 | tf_op jit(solution)/shard_map/while/body/eval_jaxpr/add | solution.py:37
  195.2 3.2 maximum_maximum_fusion.3
  198.4 17.3 %divide_add_fusion.2 = f32[32,64,64]{2,1,0:T(8,128)} fusion(f32[32,64,64]{2,1,0:T(8,128)S(1)} %copy.71, f32[32,64,64]{2,1,0:T(8,128)} %get-tuple-element.1253, f32[32,64,64]{2,1,0:T(8,128)} %get-tuple-element.1252, f32[34,66,65]{2,1,0:T(8,128)S(1)} %get-tuple-element.1079, f32[32,64,64]{2,1,0:T(8,128)} %get-tuple-element.1251, ...), kind=kLoop, calls=%fused_computation.97.clone.1 | loop fusion | flops 15073280 | bytes 25773164 | tf_op jit(solution)/shard_map/while/body/eval_jaxpr/add | solution.py:37
  234.9 3.2 maximum_maximum_fusion.3
  238.1 17.3 %divide_add_fusion.2 = f32[32,64,64]{2,1,0:T(8,128)} fusion(f32[32,64,64]{2,1,0:T(8,128)S(1)} %copy.71, f32[32,64,64]{2,1,0:T(8,128)} %get-tuple-element.1253, f32[32,64,64]{2,1,0:T(8,128)} %get-tuple-element.1252, f32[34,66,65]{2,1,0:T(8,128)S(1)} %get-tuple-element.1079, f32[32,64,64]{2,1,0:T(8,128)} %get-tuple-element.1251, ...), kind=kLoop, calls=%fused_computation.97.clone.1 | loop fusion | flops 15073280 | bytes 25773164 | tf_op jit(solution)/shard_map/while/body/eval_jaxpr/add | solution.py:37
  274.6 3.2 maximum_maximum_fusion.3
  277.8 17.3 %divide_add_fusion.2 = f32[32,64,64]{2,1,0:T(8,128)} fusion(f32[32,64,64]{2,1,0:T(8,128)S(1)} %copy.71, f32[32,64,64]{2,1,0:T(8,128)} %get-tuple-element.1253, f32[32,64,64]{2,1,0:T(8,128)} %get-tuple-element.1252, f32[34,66,65]{2,1,0:T(8,128)S(1)} %get-tuple-element.1079, f32[32,64,64]{2,1,0:T(8,128)} %get-tuple-element.1251, ...), kind=kLoop, calls=%fused_computation.97.clone.1 | loop fusion | flops 15073280 | bytes 25773164 | tf_op jit(solution)/shard_map/while/body/eval_jaxpr/add | solution.py:37
  314.3 3.2 maximum_maximum_fusion.3
  317.5 17.3 %divide_add_fusion.2 = f32[32,64,64]{2,1,0:T(8,128)} fusion(f32[32,64,64]{2,1,0:T(8,128)S(1)} %copy.71, f32[32,64,64]{2,1,0:T(8,128)} %get-tuple-element.1253, f32[32,64,64]{2,1,0:T(8,128)} %get-tuple-element.1252, f32[34,66,65]{2,1,0:T(8,128)S(1)} %get-tuple-element.1079, f32[32,64,64]{2,1,0:T(8,128)} %get-tuple-element.1251, ...), kind=kLoop, calls=%fused_computation.97.clone.1 | loop fusion | flops 15073280 | bytes 25773164 | tf_op jit(solution)/shard_map/while/body/eval_jaxpr/add | solution.py:37
  354.1 3.2 maximum_maximum_fusion.3
  357.3 17.3 %divide_add_fusion.2 = f32[32,64,64]{2,1,0:T(8,128)} fusion(f32[32,64,64]{2,1,0:T(8,128)S(1)} %copy.71, f32[32,64,64]{2,1,0:T(8,128)} %get-tuple-element.1253, f32[32,64,64]{2,1,0:T(8,128)} %get-tuple-element.1252, f32[34,66,65]{2,1,0:T(8,128)S(1)} %get-tuple-element.1079, f32[32,64,64]{2,1,0:T(8,128)} %get-tuple-element.1251, ...), kind=kLoop, calls=%fused_computation.97.clone.1 | loop fusion | flops 15073280 | bytes 25773164 | tf_op jit(solution)/shard_map/while/body/eval_jaxpr/add | solution.py:37
  393.8 3.2 maximum_maximum_fusion.3
  397.0 17.3 %divide_add_fusion.2 = f32[32,64,64]{2,1,0:T(8,128)} fusion(f32[32,64,64]{2,1,0:T(8,128)S(1)} %copy.71, f32[32,64,64]{2,1,0:T(8,128)} %get-tuple-element.1253, f32[32,64,64]{2,1,0:T(8,128)} %get-tuple-element.1252, f32[34,66,65]{2,1,0:T(8,128)S(1)} %get-tuple-element.1079, f32[32,64,64]{2,1,0:T(8,128)} %get-tuple-element.1251, ...), kind=kLoop, calls=%fused_computation.97.clone.1 | loop fusion | flops 15073280 | bytes 25773164 | tf_op jit(solution)/shard_map/while/body/eval_jaxpr/add | solution.py:37
  433.5 3.2 maximum_maximum_fusion.3
  436.7 17.3 %divide_add_fusion.2 = f32[32,64,64]{2,1,0:T(8,128)} fusion(f32[32,64,64]{2,1,0:T(8,128)S(1)} %copy.71, f32[32,64,64]{2,1,0:T(8,128)} %get-tuple-element.1253, f32[32,64,64]{2,1,0:T(8,128)} %get-tuple-element.1252, f32[34,66,65]{2,1,0:T(8,128)S(1)} %get-tuple-element.1079, f32[32,64,64]{2,1,0:T(8,128)} %get-tuple-element.1251, ...), kind=kLoop, calls=%fused_computation.97.clone.1 | loop fusion | flops 15073280 | bytes 25773164 | tf_op jit(solution)/shard_map/while/body/eval_jaxpr/add | solution.py:37
  473.2 3.2 maximum_maximum_fusion.3
  476.4 17.3 %divide_add_fusion.2 = f32[32,64,64]{2,1,0:T(8,128)} fusion(f32[32,64,64]{2,1,0:T(8,128)S(1)} %copy.71, f32[32,64,64]{2,1,0:T(8,128)} %get-tuple-element.1253, f32[32,64,64]{2,1,0:T(8,128)} %get-tuple-element.1252, f32[34,66,65]{2,1,0:T(8,128)S(1)} %get-tuple-element.1079, f32[32,64,64]{2,1,0:T(8,128)} %get-tuple-element.1251, ...), kind=kLoop, calls=%fused_computation.97.clone.1 | loop fusion | flops 15073280 | bytes 25773164 | tf_op jit(solution)/shard_map/while/body/eval_jaxpr/add | solution.py:37
  512.9 3.2 maximum_maximum_fusion.3
  516.1 17.3 %divide_add_fusion.2 = f32[32,64,64]{2,1,0:T(8,128)} fusion(f32[32,64,64]{2,1,0:T(8,128)S(1)} %copy.71, f32[32,64,64]{2,1,0:T(8,128)} %get-tuple-element.1253, f32[32,64,64]{2,1,0:T(8,128)} %get-tuple-element.1252, f32[34,66,65]{2,1,0:T(8,128)S(1)} %get-tuple-element.1079, f32[32,64,64]{2,1,0:T(8,128)} %get-tuple-element.1251, ...), kind=kLoop, calls=%fused_computation.97.clone.1 | loop fusion | flops 15073280 | bytes 25773164 | tf_op jit(solution)/shard_map/while/body/eval_jaxpr/add | solution.py:37
  552.6 3.2 maximum_maximum_fusion.3
  555.8 17.3 %divide_add_fusion.2 = f32[32,64,64]{2,1,0:T(8,128)} fusion(f32[32,64,64]{2,1,0:T(8,128)S(1)} %copy.71, f32[32,64,64]{2,1,0:T(8,128)} %get-tuple-element.1253, f32[32,64,64]{2,1,0:T(8,128)} %get-tuple-element.1252, f32[34,66,65]{2,1,0:T(8,128)S(1)} %get-tuple-element.1079, f32[32,64,64]{2,1,0:T(8,128)} %get-tuple-element.1251, ...), kind=kLoop, calls=%fused_computation.97.clone.1 | loop fusion | flops 15073280 | bytes 25773164 | tf_op jit(solution)/shard_map/while/body/eval_jaxpr/add | solution.py:37
  592.3 3.2 maximum_maximum_fusion.3
  595.5 17.3 %divide_add_fusion.2 = f32[32,64,64]{2,1,0:T(8,128)} fusion(f32[32,64,64]{2,1,0:T(8,128)S(1)} %copy.71, f32[32,64,64]{2,1,0:T(8,128)} %get-tuple-element.1253, f32[32,64,64]{2,1,0:T(8,128)} %get-tuple-element.1252, f32[34,66,65]{2,1,0:T(8,128)S(1)} %get-tuple-element.1079, f32[32,64,64]{2,1,0:T(8,128)} %get-tuple-element.1251, ...), kind=kLoop, calls=%fused_computation.97.clone.1 | loop fusion | flops 15073280 | bytes 25773164 | tf_op jit(solution)/shard_map/while/body/eval_jaxpr/add | solution.py:37
  635.2 17.3 %divide_add_fusion.2 = f32[32,64,64]{2,1,0:T(8,128)} fusion(f32[32,64,64]{2,1,0:T(8,128)S(1)} %copy.71, f32[32,64,64]{2,1,0:T(8,128)} %get-tuple-element.1253, f32[32,64,64]{2,1,0:T(8,128)} %get-tuple-element.1252, f32[34,66,65]{2,1,0:T(8,128)S(1)} %get-tuple-element.1079, f32[32,64,64]{2,1,0:T(8,128)} %get-tuple-element.1251, ...), kind=kLoop, calls=%fused_computation.97.clone.1 | loop fusion | flops 15073280 | bytes 25773164 | tf_op jit(solution)/shard_map/while/body/eval_jaxpr/add | solution.py:37
  671.8 3.2 maximum_maximum_fusion.3
  675.0 17.3 %divide_add_fusion.2 = f32[32,64,64]{2,1,0:T(8,128)} fusion(f32[32,64,64]{2,1,0:T(8,128)S(1)} %copy.71, f32[32,64,64]{2,1,0:T(8,128)} %get-tuple-element.1253, f32[32,64,64]{2,1,0:T(8,128)} %get-tuple-element.1252, f32[34,66,65]{2,1,0:T(8,128)S(1)} %get-tuple-element.1079, f32[32,64,64]{2,1,0:T(8,128)} %get-tuple-element.1251, ...), kind=kLoop, calls=%fused_computation.97.clone.1 | loop fusion | flops 15073280 | bytes 25773164 | tf_op jit(solution)/shard_map/while/body/eval_jaxpr/add | solution.py:37
  711.5 3.2 maximum_maximum_fusion.3
  714.7 17.3 %divide_add_fusion.2 = f32[32,64,64]{2,1,0:T(8,128)} fusion(f32[32,64,64]{2,1,0:T(8,128)S(1)} %copy.71, f32[32,64,64]{2,1,0:T(8,128)} %get-tuple-element.1253, f32[32,64,64]{2,1,0:T(8,128)} %get-tuple-element.1252, f32[34,66,65]{2,1,0:T(8,128)S(1)} %get-tuple-element.1079, f32[32,64,64]{2,1,0:T(8,128)} %get-tuple-element.1251, ...), kind=kLoop, calls=%fused_computation.97.clone.1 | loop fusion | flops 15073280 | bytes 25773164 | tf_op jit(solution)/shard_map/while/body/eval_jaxpr/add | solution.py:37
  751.2 3.2 maximum_maximum_fusion.3
  754.4 17.3 %divide_add_fusion.2 = f32[32,64,64]{2,1,0:T(8,128)} fusion(f32[32,64,64]{2,1,0:T(8,128)S(1)} %copy.71, f32[32,64,64]{2,1,0:T(8,128)} %get-tuple-element.1253, f32[32,64,64]{2,1,0:T(8,128)} %get-tuple-element.1252, f32[34,66,65]{2,1,0:T(8,128)S(1)} %get-tuple-element.1079, f32[32,64,64]{2,1,0:T(8,128)} %get-tuple-element.1251, ...), kind=kLoop, calls=%fused_computation.97.clone.1 | loop fusion | flops 15073280 | bytes 25773164 | tf_op jit(solution)/shard_map/while/body/eval_jaxpr/add | solution.py:37
  790.9 3.2 maximum_maximum_fusion.3
  794.1 17.3 %divide_add_fusion.2 = f32[32,64,64]{2,1,0:T(8,128)} fusion(f32[32,64,64]{2,1,0:T(8,128)S(1)} %copy.71, f32[32,64,64]{2,1,0:T(8,128)} %get-tuple-element.1253, f32[32,64,64]{2,1,0:T(8,128)} %get-tuple-element.1252, f32[34,66,65]{2,1,0:T(8,128)S(1)} %get-tuple-element.1079, f32[32,64,64]{2,1,0:T(8,128)} %get-tuple-element.1251, ...), kind=kLoop, calls=%fused_computation.97.clone.1 | loop fusion | flops 15073280 | bytes 25773164 | tf_op jit(solution)/shard_map/while/body/eval_jaxpr/add | solution.py:37
  830.6 3.2 maximum_maximum_fusion.3
  833.8 17.3 %divide_add_fusion.2 = f32[32,64,64]{2,1,0:T(8,128)} fusion(f32[32,64,64]{2,1,0:T(8,128)S(1)} %copy.71, f32[32,64,64]{2,1,0:T(8,128)} %get-tuple-element.1253, f32[32,64,64]{2,1,0:T(8,128)} %get-tuple-element.1252, f32[34,66,65]{2,1,0:T(8,128)S(1)} %get-tuple-element.1079, f32[32,64,64]{2,1,0:T(8,128)} %get-tuple-element.1251, ...), kind=kLoop, calls=%fused_computation.97.clone.1 | loop fusion | flops 15073280 | bytes 25773164 | tf_op jit(solution)/shard_map/while/body/eval_jaxpr/add | solution.py:37
  870.3 3.2 maximum_maximum_fusion.3
  873.5 17.3 %divide_add_fusion.2 = f32[32,64,64]{2,1,0:T(8,128)} fusion(f32[32,64,64]{2,1,0:T(8,128)S(1)} %copy.71, f32[32,64,64]{2,1,0:T(8,128)} %get-tuple-element.1253, f32[32,64,64]{2,1,0:T(8,128)} %get-tuple-element.1252, f32[34,66,65]{2,1,0:T(8,128)S(1)} %get-tuple-element.1079, f32[32,64,64]{2,1,0:T(8,128)} %get-tuple-element.1251, ...), kind=kLoop, calls=%fused_computation.97.clone.1 | loop fusion | flops 15073280 | bytes 25773164 | tf_op jit(solution)/shard_map/while/body/eval_jaxpr/add | solution.py:37
  910.0 3.2 maximum_maximum_fusion.3
  913.2 17.3 %divide_add_fusion.2 = f32[32,64,64]{2,1,0:T(8,128)} fusion(f32[32,64,64]{2,1,0:T(8,128)S(1)} %copy.71, f32[32,64,64]{2,1,0:T(8,128)} %get-tuple-element.1253, f32[32,64,64]{2,1,0:T(8,128)} %get-tuple-element.1252, f32[34,66,65]{2,1,0:T(8,128)S(1)} %get-tuple-element.1079, f32[32,64,64]{2,1,0:T(8,128)} %get-tuple-element.1251, ...), kind=kLoop, calls=%fused_computation.97.clone.1 | loop fusion | flops 15073280 | bytes 25773164 | tf_op jit(solution)/shard_map/while/body/eval_jaxpr/add | solution.py:37
  949.7 3.2 maximum_maximum_fusion.3
  953.0 17.3 %divide_add_fusion.2 = f32[32,64,64]{2,1,0:T(8,128)} fusion(f32[32,64,64]{2,1,0:T(8,128)S(1)} %copy.71, f32[32,64,64]{2,1,0:T(8,128)} %get-tuple-element.1253, f32[32,64,64]{2,1,0:T(8,128)} %get-tuple-element.1252, f32[34,66,65]{2,1,0:T(8,128)S(1)} %get-tuple-element.1079, f32[32,64,64]{2,1,0:T(8,128)} %get-tuple-element.1251, ...), kind=kLoop, calls=%fused_computation.97.clone.1 | loop fusion | flops 15073280 | bytes 25773164 | tf_op jit(solution)/shard_map/while/body/eval_jaxpr/add | solution.py:37
  992.7 17.3 %divide_add_fusion.2 = f32[32,64,64]{2,1,0:T(8,128)} fusion(f32[32,64,64]{2,1,0:T(8,128)S(1)} %copy.71, f32[32,64,64]{2,1,0:T(8,128)} %get-tuple-element.1253, f32[32,64,64]{2,1,0:T(8,128)} %get-tuple-element.1252, f32[34,66,65]{2,1,0:T(8,128)S(1)} %get-tuple-element.1079, f32[32,64,64]{2,1,0:T(8,128)} %get-tuple-element.1251, ...), kind=kLoop, calls=%fused_computation.97.clone.1 | loop fusion | flops 15073280 | bytes 25773164 | tf_op jit(solution)/shard_map/while/body/eval_jaxpr/add | solution.py:37
  1032.4 17.3 %divide_add_fusion.2 = f32[32,64,64]{2,1,0:T(8,128)} fusion(f32[32,64,64]{2,1,0:T(8,128)S(1)} %copy.71, f32[32,64,64]{2,1,0:T(8,128)} %get-tuple-element.1253, f32[32,64,64]{2,1,0:T(8,128)} %get-tuple-element.1252, f32[34,66,65]{2,1,0:T(8,128)S(1)} %get-tuple-element.1079, f32[32,64,64]{2,1,0:T(8,128)} %get-tuple-element.1251, ...), kind=kLoop, calls=%fused_computation.97.clone.1 | loop fusion | flops 15073280 | bytes 25773164 | tf_op jit(solution)/shard_map/while/body/eval_jaxpr/add | solution.py:37
  1068.9 3.2 maximum_maximum_fusion.3
  1072.1 17.3 %divide_add_fusion.2 = f32[32,64,64]{2,1,0:T(8,128)} fusion(f32[32,64,64]{2,1,0:T(8,128)S(1)} %copy.71, f32[32,64,64]{2,1,0:T(8,128)} %get-tuple-element.1253, f32[32,64,64]{2,1,0:T(8,128)} %get-tuple-element.1252, f32[34,66,65]{2,1,0:T(8,128)S(1)} %get-tuple-element.1079, f32[32,64,64]{2,1,0:T(8,128)} %get-tuple-element.1251, ...), kind=kLoop, calls=%fused_computation.97.clone.1 | loop fusion | flops 15073280 | bytes 25773164 | tf_op jit(solution)/shard_map/while/body/eval_jaxpr/add | solution.py:37
  1108.6 3.2 maximum_maximum_fusion.3
  1111.8 17.3 %divide_add_fusion.2 = f32[32,64,64]{2,1,0:T(8,128)} fusion(f32[32,64,64]{2,1,0:T(8,128)S(1)} %copy.71, f32[32,64,64]{2,1,0:T(8,128)} %get-tuple-element.1253, f32[32,64,64]{2,1,0:T(8,128)} %get-tuple-element.1252, f32[34,66,65]{2,1,0:T(8,128)S(1)} %get-tuple-element.1079, f32[32,64,64]{2,1,0:T(8,128)} %get-tuple-element.1251, ...), kind=kLoop, calls=%fused_computation.97.clone.1 | loop fusion | flops 15073280 | bytes 25773164 | tf_op jit(solution)/shard_map/while/body/eval_jaxpr/add | solution.py:37
  1148.3 3.2 maximum_maximum_fusion.3
  1151.5 17.3 %divide_add_fusion.2 = f32[32,64,64]{2,1,0:T(8,128)} fusion(f32[32,64,64]{2,1,0:T(8,128)S(1)} %copy.71, f32[32,64,64]{2,1,0:T(8,128)} %get-tuple-element.1253, f32[32,64,64]{2,1,0:T(8,128)} %get-tuple-element.1252, f32[34,66,65]{2,1,0:T(8,128)S(1)} %get-tuple-element.1079, f32[32,64,64]{2,1,0:T(8,128)} %get-tuple-element.1251, ...), kind=kLoop, calls=%fused_computation.97.clone.1 | loop fusion | flops 15073280 | bytes 25773164 | tf_op jit(solution)/shard_map/while/body/eval_jaxpr/add | solution.py:37
  1188.0 3.2 maximum_maximum_fusion.3
  1191.2 17.3 %divide_add_fusion.2 = f32[32,64,64]{2,1,0:T(8,128)} fusion(f32[32,64,64]{2,1,0:T(8,128)S(1)} %copy.71, f32[32,64,64]{2,1,0:T(8,128)} %get-tuple-element.1253, f32[32,64,64]{2,1,0:T(8,128)} %get-tuple-element.1252, f32[34,66,65]{2,1,0:T(8,128)S(1)} %get-tuple-element.1079, f32[32,64,64]{2,1,0:T(8,128)} %get-tuple-element.1251, ...), kind=kLoop, calls=%fused_computation.97.clone.1 | loop fusion | flops 15073280 | bytes 25773164 | tf_op jit(solution)/shard_map/while/body/eval_jaxpr/add | solution.py:37
  1227.7 3.2 maximum_maximum_fusion.3
  1230.9 17.3 %divide_add_fusion.2 = f32[32,64,64]{2,1,0:T(8,128)} fusion(f32[32,64,64]{2,1,0:T(8,128)S(1)} %copy.71, f32[32,64,64]{2,1,0:T(8,128)} %get-tuple-element.1253, f32[32,64,64]{2,1,0:T(8,128)} %get-tuple-element.1252, f32[34,66,65]{2,1,0:T(8,128)S(1)} %get-tuple-element.1079, f32[32,64,64]{2,1,0:T(8,128)} %get-tuple-element.1251, ...), kind=kLoop, calls=%fused_computation.97.clone.1 | loop fusion | flops 15073280 | bytes 25773164 | tf_op jit(solution)/shard_map/while/body/eval_jaxpr/add | solution.py:37
  1267.5 3.2 maximum_maximum_fusion.3
  1270.7 17.3 %divide_add_fusion.2 = f32[32,64,64]{2,1,0:T(8,128)} fusion(f32[32,64,64]{2,1,0:T(8,128)S(1)} %copy.71, f32[32,64,64]{2,1,0:T(8,128)} %get-tuple-element.1253, f32[32,64,64]{2,1,0:T(8,128)} %get-tuple-element.1252, f32[34,66,65]{2,1,0:T(8,128)S(1)} %get-tuple-element.1079, f32[32,64,64]{2,1,0:T(8,128)} %get-tuple-element.1251, ...), kind=kLoop, calls=%fused_computation.97.clone.1 | loop fusion | flops 15073280 | bytes 25773164 | tf_op jit(solution)/shard_map/while/body/eval_jaxpr/add | solution.py:37
  1307.2 3.2 maximum_maximum_fusion.3
  1310.4 17.3 %divide_add_fusion.2 = f32[32,64,64]{2,1,0:T(8,128)} fusion(f32[32,64,64]{2,1,0:T(8,128)S(1)} %copy.71, f32[32,64,64]{2,1,0:T(8,128)} %get-tuple-element.1253, f32[32,64,64]{2,1,0:T(8,128)} %get-tuple-element.1252, f32[34,66,65]{2,1,0:T(8,128)S(1)} %get-tuple-element.1079, f32[32,64,64]{2,1,0:T(8,128)} %get-tuple-element.1251, ...), kind=kLoop, calls=%fused_computation.97.clone.1 | loop fusion | flops 15073280 | bytes 25773164 | tf_op jit(solution)/shard_map/while/body/eval_jaxpr/add | solution.py:37
  (1229 shorter events, 643.4 us)
Async XLA Ops:
  5.8 3.9 collective-permute-start.8
  12.5 21.3 %collective-permute-start.10 = (f32[34,66,1]{1,2,0:T(1,128)}, f32[34,66,1]{1,2,0:T(1,128)S(1)}, u32[]{:S(2)}, u32[]{:S(2)}) collective-permute-start(f32[34,66,1]{1,2,0:T(1,128)} %copy.44), channel_id=1, source_target_pairs={{0,8},{8,16},{16,24},{24,0},{1,9},{9,17},{17,25},{25,1},{2,10},{10... | collective-permute-start | bytes 26936 | tf_op jit(solution)/shard_map/ppermute | solution.py:46
  14.5 20.9 %collective-permute-start.11 = (f32[34,66,1]{1,2,0:T(1,128)S(1)}, f32[34,66,1]{1,2,0:T(1,128)S(1)}, u32[]{:S(2)}, u32[]{:S(2)}) collective-permute-start(f32[34,66,1]{1,2,0:T(1,128)S(1)} %copy.46), channel_id=1, source_target_pairs={{0,24},{8,0},{16,8},{24,16},{1,25},{9,1},{17,9},{25,17},{2,26},{10... | collective-permute-start | bytes 26936 | tf_op jit(solution)/shard_map/ppermute | solution.py:47
  69.1 3.8 collective-permute-start.4
  69.6 4.9 collective-permute-start.5
  108.8 3.8 collective-permute-start.4
  109.3 4.9 collective-permute-start.5
  142.5 3.8 collective-permute-start.3
  148.6 3.8 collective-permute-start.4
  149.0 4.9 collective-permute-start.5
  182.2 3.8 collective-permute-start.3
  188.3 3.8 collective-permute-start.4
  188.7 4.9 collective-permute-start.5
  221.9 3.8 collective-permute-start.3
  228.4 4.9 collective-permute-start.5
  261.6 3.8 collective-permute-start.3
  268.1 4.9 collective-permute-start.5
  301.3 3.8 collective-permute-start.3
  307.9 4.9 collective-permute-start.5
  341.1 3.8 collective-permute-start.3
  347.1 3.8 collective-permute-start.4
  347.6 4.9 collective-permute-start.5
  386.8 3.8 collective-permute-start.4
  387.3 4.9 collective-permute-start.5
  426.5 3.8 collective-permute-start.4
  427.0 4.9 collective-permute-start.5
  466.3 3.8 collective-permute-start.4
  466.7 4.9 collective-permute-start.5
  499.9 3.8 collective-permute-start.3
  506.0 3.8 collective-permute-start.4
  506.4 4.9 collective-permute-start.5
  539.6 3.8 collective-permute-start.3
  545.7 3.8 collective-permute-start.4
  546.1 4.9 collective-permute-start.5
  579.3 3.8 collective-permute-start.3
  585.9 4.9 collective-permute-start.5
  619.0 3.8 collective-permute-start.3
  625.6 4.9 collective-permute-start.5
  658.8 3.8 collective-permute-start.3
  665.3 4.9 collective-permute-start.5
  698.5 3.8 collective-permute-start.3
  705.0 4.9 collective-permute-start.5
  744.2 3.8 collective-permute-start.4
  744.7 4.9 collective-permute-start.5
  784.0 3.8 collective-permute-start.4
  784.4 4.9 collective-permute-start.5
  823.7 3.8 collective-permute-start.4
  824.1 4.9 collective-permute-start.5
  863.4 3.8 collective-permute-start.4
  863.8 4.9 collective-permute-start.5
  897.0 3.8 collective-permute-start.3
  903.1 3.8 collective-permute-start.4
  903.6 4.9 collective-permute-start.5
  936.8 3.8 collective-permute-start.3
  943.3 4.9 collective-permute-start.5
  983.0 4.9 collective-permute-start.5
  1022.7 4.9 collective-permute-start.5
  1062.4 4.9 collective-permute-start.5
  1102.1 4.9 collective-permute-start.5
  1141.8 4.9 collective-permute-start.5
  1181.6 4.9 collective-permute-start.5
  1221.3 4.9 collective-permute-start.5
  1261.0 4.9 collective-permute-start.5
  1300.7 4.9 collective-permute-start.5
  (334 other events, 842.4 us)
where the time goes:
time: 1330 us
  other arithmetic  680 us (51%)
  local copies, waits for them, and re-layouts  274 us (21%)
  starting transfers between devices  243 us (18%)
  waiting for transfers between devices  112 us (8%)
  between operations  16.3 us (1%)
    add x32, other arithmetic, jacobi_step(): return u_mid + relax_now * (f_reg - applied) / diag_reg  553 us
    ppermute x99, starting transfers between devices, halo_axis(): from_prev = lax.ppermute(high_part, axis_name, to_next)  132 us
    concatenate x66, other arithmetic, halo_axis(): return jnp.concatenate([from_prev, brick_in, from_next], axis=axis_dim)  111 us
    ppermute x99, starting transfers between devices, halo_axis(): from_next = lax.ppermute(low_part, axis_name, to_prev)  110 us
    while x480, local copies, waits for them, and re-layouts  81.6 us
    ppermute x99, waiting for transfers between devices, halo_axis(): from_prev = lax.ppermute(high_part, axis_name, to_next)  75.4 us
    ppermute x33, local copies, waits for them, and re-layouts, halo_axis(): from_prev = lax.ppermute(high_part, axis_name, to_next)  51.6 us
    ppermute x33, local copies, waits for them, and re-layouts, halo_axis(): from_next = lax.ppermute(low_part, axis_name, to_prev)  51.3 us
  transfers between devices with their start and end apart: 198, of which 99 were waited for; matrix products, arithmetic and copies ran while one was open for 7% of the time, Pallas kernels for 0%

commit v1 on v0

v1 whole, which is shorter than its diff:
```python
import functools

import jax
import jax.numpy as jnp
from jax import lax
from jax.experimental import pallas as pl
from jax.experimental.pallas import tpu as pltpu
from jax.sharding import PartitionSpec as P

MESH = pl.DeviceIdType.MESH
F32 = jnp.float32
DEPTH = 4
ROW0 = 8
LANES = 128

OFFSETS = [(b, c, a) for a in (-1, 0, 1) for b in (-1, 0, 1) for c in (-1, 0, 1) if (a, b, c) != (0, 0, 0)]


def lane_of(shape):
    return lax.broadcasted_iota(jnp.int32, shape, len(shape) - 1)


def shift_x(v, c, half):
    lane = lane_of(v.shape) % half
    if c == 1:
        return jnp.where(lane == half - 1, pltpu.roll(v, half - 1, 1), pltpu.roll(v, 2 * half - 1, 1))
    return jnp.where(lane == 0, pltpu.roll(v, half + 1, 1), pltpu.roll(v, 1, 1))


def kernel(dims, u_in, f_in, k_in, w_ref, om_ref, out_ref,
           start0, start1, temp, kap, frc, coef, zsend, zrecv, drecv, send_sem, recv_sem):
    n_y, n_z, ny, nz, sweeps, tiles = dims
    s = DEPTH
    half = LANES // 2
    lo, hi = ROW0, ROW0 + nz
    qe = ny + 2 * s
    first = lo - s + 1

    core = lax.axis_index("gx")
    gy = lax.axis_index("gy")
    gz = lax.axis_index("gz")
    zhi, zlo = lax.rem(gz + 1, n_z), lax.rem(gz + n_z - 1, n_z)
    other = 1 - core
    yhi = lax.rem(gy + core, n_y)
    ylo = lax.rem(gy + n_y - other, n_y)

    def dev(y, z):
        if y is None:
            return {"gz": z}
        if z is None:
            return {"gx": other, "gy": y}
        return {"gx": other, "gy": y, "gz": z}

    neighbours = [dev(yhi, None), dev(ylo, None), dev(None, zhi), dev(None, zlo),
                  dev(yhi, zhi), dev(ylo, zhi), dev(yhi, zlo), dev(ylo, zlo)]

    barrier = pltpu.get_barrier_semaphore()
    for nb in neighbours:
        pl.semaphore_signal(barrier, inc=1, device_id=nb, device_id_type=MESH)

    hq = ny // 2

    def copies(arr, slot):
        pieces = [
            (arr.at[pl.ds(ny, s), pl.ds(lo, nz)], arr.at[pl.ds(0, s), pl.ds(lo, nz)]),
            (arr.at[pl.ds(s, s), pl.ds(lo, nz)], arr.at[pl.ds(ny + s, s), pl.ds(lo, nz)]),
            (zsend.at[slot, 0], zrecv.at[slot, 0]),
            (zsend.at[slot, 1], zrecv.at[slot, 1]),
            (zsend.at[slot, 0, pl.ds((hq - s) * s, s * s)], drecv.at[slot, 0]),
            (zsend.at[slot, 0, pl.ds(0, s * s)], drecv.at[slot, 1]),
            (zsend.at[slot, 1, pl.ds((hq - s) * s, s * s)], drecv.at[slot, 2]),
            (zsend.at[slot, 1, pl.ds(0, s * s)], drecv.at[slot, 3]),
        ]
        return [
            pltpu.make_async_remote_copy(
                src_ref=src, dst_ref=dst, send_sem=send_sem.at[slot, i], recv_sem=recv_sem.at[slot, i],
                device_id=neighbours[i], device_id_type=MESH)
            for i, (src, dst) in enumerate(pieces)
        ]

    left = lane_of((s, LANES)) < half

    def swap(v):
        return pltpu.roll(v, half, 1)

    def begin(arr, slot):
        for q in range(hq):
            top = jnp.where(left, swap(arr[s + q, pl.ds(hi - s, s)]), arr[s + q + hq, pl.ds(hi - s, s)])
            zsend[slot, 0, pl.ds(q * s, s)] = top
            bottom = jnp.where(left, arr[s + q, pl.ds(lo, s)], swap(arr[s + q + hq, pl.ds(lo, s)]))
            zsend[slot, 1, pl.ds(q * s, s)] = bottom
        for cp in copies(arr, slot):
            cp.start()

    def finish(arr, slot):
        for cp in copies(arr, slot):
            cp.wait()
        for q in range(qe):
            if q < s:
                low = swap(drecv[slot, 0, pl.ds(q * s, s)])
                high = drecv[slot, 2, pl.ds(q * s, s)]
            elif q < s + hq:
                low = zrecv[slot, 0, pl.ds((q - s) * s, s)]
                high = swap(zrecv[slot, 1, pl.ds((q - s) * s, s)])
            elif q < s + ny:
                low = swap(zrecv[slot, 0, pl.ds((q - s - hq) * s, s)])
                high = zrecv[slot, 1, pl.ds((q - s - hq) * s, s)]
            else:
                low = drecv[slot, 1, pl.ds((q - s - ny) * s, s)]
                high = swap(drecv[slot, 3, pl.ds((q - s - ny) * s, s)])
            arr[q, pl.ds(lo - s, s)] = jnp.where(left, low, swap(arr[q, pl.ds(hi - s, s)]))
            arr[q, pl.ds(hi, s)] = jnp.where(left, swap(arr[q, pl.ds(lo, s)]), high)

    for arr, src in ((start0, u_in), (kap, k_in), (frc, f_in)):
        @pl.loop(0, ny)
        def _(q, arr=arr, src=src):
            arr[s + q, pl.ds(lo, nz)] = src[q]
    pl.semaphore_wait(barrier, len(neighbours))
    begin(kap, 2)
    begin(frc, 3)
    begin(start0, 0)
    finish(kap, 2)
    finish(frc, 3)

    @pl.loop(1, qe - 1)
    def _(q):
        for t in range(tiles):
            base = first + 8 * t
            k_ab = {(a, b): kap[q + a, pl.ds(base + b, 8)] for a in (-1, 0, 1) for b in (-1, 0, 1)}
            k_mid = k_ab[0, 0]
            mids = {0: k_mid, 1: shift_x(k_mid, -1, half), -1: shift_x(k_mid, 1, half)}
            raw, sums = [], {}
            for m, (a, b, c) in enumerate(OFFSETS):
                d = (0.5 * w_ref[m]) * (mids[c] + k_ab[a, b])
                raw.append(d)
                sums[c] = d if c not in sums else sums[c] + d
            diag = sums[0] + shift_x(sums[1], 1, half) + shift_x(sums[-1], -1, half)
            inv = 1.0 / diag
            invs = {0: inv, 1: shift_x(inv, -1, half), -1: shift_x(inv, 1, half)}
            idx = (q - 1) * tiles + t
            for m, (a, b, c) in enumerate(OFFSETS):
                coef[idx, m] = raw[m] * invs[c]
            coef[idx, len(OFFSETS)] = frc[q, pl.ds(base, 8)] * inv

    BLOCK = 2

    def sweep(src, dst, j, relax):
        @pl.loop(0, (qe - 2 - 2 * j) // BLOCK)
        def _(blk):
            q0 = 1 + j + blk * BLOCK
            for t in range(tiles):
                base = first + 8 * t
                rows = {(i, b): src[q0 - 1 + i, pl.ds(base + b, 8)] for i in range(BLOCK + 2) for b in (-1, 0, 1)}
                for i in range(BLOCK):
                    idx = (q0 + i - 1) * tiles + t
                    sums = {0: coef[idx, len(OFFSETS)]}
                    for m, (a, b, c) in enumerate(OFFSETS):
                        p = coef[idx, m] * rows[i + 1 + a, b]
                        sums[c] = p if c not in sums else sums[c] + p
                    total = sums[0] + shift_x(sums[1], 1, half) + shift_x(sums[-1], -1, half)
                    mid = rows[i + 1, 0]
                    dst[q0 + i, pl.ds(base, 8)] = mid + relax * (total - mid)

    def group(arr, nxt, k0):
        bufs = [arr, temp]
        for j in range(s):
            dst = nxt if j == s - 1 else bufs[(j + 1) % 2]
            sweep(bufs[j % 2], dst, j, om_ref[k0 + j])

    groups = sweeps // s

    @pl.loop(0, groups // 2)
    def _(i):
        finish(start0, 0)
        group(start0, start1, 2 * s * i)
        begin(start1, 1)
        finish(start1, 1)
        group(start1, start0, 2 * s * i + s)

        @pl.when(i < groups // 2 - 1)
        def _():
            begin(start0, 0)

    @pl.loop(0, ny)
    def _(q):
        out_ref[q] = start0[s + q, pl.ds(lo, nz)]


def solution(mesh):
    spec = P(("batch", "gx"), "gy", "gz")
    n_x, n_y, n_z = mesh.shape["gx"], mesh.shape["gy"], mesh.shape["gz"]

    def local(u, f, k, w, om):
        bx, by, bz = u.shape
        ny, nz = by // n_x, bz // 2
        s = DEPTH
        tiles = -(-(nz + 2 * s - 2) // 8)
        rows = ROW0 + -(-(nz + s) // 8) * 8
        qe = ny + 2 * s

        def to_lanes(v):
            v = lax.all_to_all(v, "gx", 2, 1, tiled=True)
            v = v.reshape(3, bx * n_x, ny, 2, nz)
            return v.transpose(0, 2, 4, 3, 1).reshape(3, ny, nz, LANES)

        def from_lanes(v):
            v = v.reshape(ny, nz, 2, bx * n_x).transpose(3, 0, 2, 1).reshape(bx * n_x, ny, bz)
            return lax.all_to_all(v, "gx", 0, 1, tiled=True)

        packed = to_lanes(jnp.stack([u, f, k]))
        vm = pl.BlockSpec(memory_space=pltpu.VMEM)
        sm = pl.BlockSpec(memory_space=pltpu.SMEM)
        arr = pltpu.VMEM((qe, rows, LANES), F32)
        out = pl.pallas_call(
            functools.partial(kernel, (n_y, n_z, ny, nz, om.shape[0], tiles)),
            out_shape=jax.ShapeDtypeStruct((ny, nz, LANES), F32),
            in_specs=[vm, vm, vm, sm, sm],
            out_specs=vm,
            scratch_shapes=[
                arr, arr, arr, arr, arr,
                pltpu.VMEM(((qe - 2) * tiles, len(OFFSETS) + 1, 8, LANES), F32),
                pltpu.VMEM((4, 2, ny // 2 * s, LANES), F32),
                pltpu.VMEM((4, 2, ny // 2 * s, LANES), F32),
                pltpu.VMEM((4, 4, s * s, LANES), F32),
                pltpu.SemaphoreType.DMA((4, 8)),
                pltpu.SemaphoreType.DMA((4, 8)),
            ],
            compiler_params=pltpu.CompilerParams(collective_id=0, has_side_effects=True, vmem_limit_bytes=56 << 20),
        )(packed[0], packed[1], packed[2], w, om)
        return from_lanes(out)

    return jax.shard_map(local, mesh=mesh, in_specs=(spec, spec, spec, P(), P()), out_specs=spec, check_vma=False)
```

time: 1330 us -> 206 us (0.15)
  other arithmetic: 680 us -> 9.32 us
  starting transfers between devices: 243 us -> 0 us
  local copies, waits for them, and re-layouts: 274 us -> 42.5 us
  Pallas kernels: 0 us -> 140 us
  waiting for transfers between devices: 112 us -> 0 us
  between operations: 16.3 us -> 0.09 us
  blocking collectives: 0 us -> 13.9 us
    add x33 -> x0, other arithmetic: 569 us -> none  [the longest x32 553 us: jacobi_step(): return u_mid + relax_now * (f_reg - applied) / diag_reg]
    ppermute x198 -> x0, starting transfers between devices: 243 us -> none  [the longest x99 132 us: halo_axis(): from_prev = lax.ppermute(high_part, axis_name, to_next)]
    pallas_call x0 -> x1, Pallas kernels: none -> 140 us  [local(): pl.pallas_call(functools.partial(kernel, (n_y, n_z, ny, nz, om.shape[0],...]
    ppermute x198 -> x0, waiting for transfers between devices: 112 us -> none  [the longest x99 75.4 us: halo_axis(): from_prev = lax.ppermute(high_part, axis_name, to_next)]
    concatenate x66 -> x0, other arithmetic: 111 us -> none  [halo_axis(): return jnp.concatenate([from_prev, brick_in, from_next], axis=axis_dim)]
    ppermute x66 -> x0, local copies, waits for them, and re-layouts: 103 us -> none  [the longest x33 51.6 us: halo_axis(): from_prev = lax.ppermute(high_part, axis_name, to_next)]
    while x480 -> x0, local copies, waits for them, and re-layouts: 81.6 us -> none
    slice x167 -> x4, local copies, waits for them, and re-layouts: 65.8 us -> 11.4 us  [the longest x2 7.37 us: local(): packed[2]]
  transfers between devices with their start and end apart: 198 -> 0, of which waited for: 99 -> 0; matrix products, arithmetic and copies ran while one was open for 7% -> 0% of each run, Pallas kernels for 0% -> 0%
where the time goes in v1:
time: 206 us; the launch traced here: 205 us
  Pallas kernels  140 us (68%)
  local copies, waits for them, and re-layouts  42.5 us (21%)
  blocking collectives  13.9 us (7%)
  other arithmetic  9.32 us (5%)
    pallas_call x1, Pallas kernels, local(): pl.pallas_call(functools.partial(kernel, (n_y, n_z, ny, nz, om.shape[0],...  140 us
    unnamed x5, local copies, waits for them, and re-layouts  9.18 us
    all_to_all x1, blocking collectives, to_lanes(): v = lax.all_to_all(v, 'gx', 2, 1, tiled=True)  7.69 us
    slice x2, local copies, waits for them, and re-layouts, local(): packed[2]  7.37 us
    reshape x1, local copies, waits for them, and re-layouts, to_lanes(): v = v.reshape(3, bx * n_x, ny, 2, nz)  7.11 us
    all_to_all x1, other arithmetic, to_lanes(): v = lax.all_to_all(v, 'gx', 2, 1, tiled=True)  6.64 us
    all_to_all x1, blocking collectives, from_lanes(): return lax.all_to_all(v, 'gx', 0, 1, tiled=True)  6.25 us

profile of v1, /device:TPU:97, one launch (start us, length us, event | category | flops | bytes accessed | tf_op | source)
XLA Modules:
  0.0 205.4 jit_solution(11703695951492713965)
XLA Ops:
  0.0 1.8 copy.34
  1.8 2.8 %copy_bitcast_fusion.1 = (f32[1,32,64,64]{3,1,0,2:T(8,128)S(1)}, f32[1,32,64,64]{3,1,0,2:T(8,128)S(1)}) fusion(f32[32,64,64]{2,1,0:T(8,128)} %param.7, f32[32,64,64]{2,1,0:T(8,128)} %param.6), kind=kLoop, calls=%fused_computation.2 | loop fusion | bytes 2097152 | tf_op jit(solution)/shard_map/stack | solution.py:210
  4.6 0.4 fusion.1
  5.0 2.9 %reshape.20 = f32[2,1,196608]{2,1,0:T(1,128)} reshape(f32[64,3,32,64]{3,2,1,0:T(8,128)S(1)} %fusion.1) | data formatting | bytes 3145728
  7.9 7.7 %all_to_all.33 = f32[2,1,196608]{2,1,0:T(1,128)S(1)} all-to-all(f32[2,1,196608]{2,1,0:T(1,128)} %reshape.20), channel_id=1, replica_groups=mesh['batch'=1,'gz'=4,'gy'=4,'gx'=2] {'gx'}, dimensions={0} | all-to-all | bytes 3145728 | tf_op jit(solution)/shard_map/all_to_all | solution.py:202
  15.6 0.6 broadcast
  16.1 6.6 %reduce = f32[2,196608]{1,0:T(2,128)} reduce(f32[2,1,196608]{2,1,0:T(1,128)S(1)} %all_to_all.33, f32[]{:T(128)} %broadcast), dimensions={1}, to_apply=%all_to_all.24.reduce_sub_computation | reduce | bytes 3145732 | tf_op jit(solution)/shard_map/all_to_all | solution.py:202
  22.8 3.1 %reshape.21 = f32[64,3,32,64]{3,2,1,0:T(8,128)S(1)} reshape(f32[2,196608]{1,0:T(2,128)} %reduce) | data formatting | bytes 3145728
  25.9 3.5 %copy.33 = f32[3,32,2,32,64]{4,3,1,2,0:T(8,128)} copy(f32[3,32,2,32,64]{4,1,0,3,2:T(8,128)S(1)} %bitcast.25) | data formatting | bytes 3145728 | tf_op jit(solution)/shard_map/all_to_all | solution.py:202
  29.4 7.1 %reshape.17 = f32[3,64,32,2,32]{4,3,2,1,0:T(2,128)} reshape(f32[3,2,32,32,64]{4,3,2,1,0:T(8,128)} %bitcast.26) | data formatting | bytes 3145728 | tf_op jit(solution)/shard_map/reshape | solution.py:203
  36.5 4.5 %fusion = (f32[1,32,32,2,64]{2,3,1,4,0:T(2,128)}, f32[1,32,32,2,64]{2,3,1,4,0:T(2,128)}, f32[1,32,32,2,64]{2,3,1,4,0:T(2,128)S(1)}) fusion(f32[3,32,32,2,64]{2,3,1,4,0:T(2,128)} %bitcast.24), kind=kLoop, calls=%fused_computation.5 | loop fusion | bytes 3145728 | tf_op jit(solution)/shard_map/slice | solution.py:229
  41.0 2.9 %copy.25 = f32[1,32,32,2,64]{4,3,2,1,0:T(2,128)S(1)} copy(f32[1,32,32,2,64]{2,3,1,4,0:T(2,128)} %get-tuple-element.5) | data formatting | bytes 1048576 | tf_op jit(solution)/shard_map/slice | solution.py:229
  43.9 1.4 squeeze.11.k_in
  45.3 2.9 %copy.24 = f32[1,32,32,2,64]{4,3,2,1,0:T(2,128)S(1)} copy(f32[1,32,32,2,64]{2,3,1,4,0:T(2,128)} %get-tuple-element.6) | data formatting | bytes 1048576 | tf_op jit(solution)/shard_map/slice | solution.py:229
  48.2 1.4 squeeze.10.f_in
  49.6 1.2 copy.23
  50.8 1.4 squeeze.9.u_in
  52.2 139.6 %shard_map.55 = f32[32,32,128]{2,1,0:T(8,128)} custom-call(f32[32,32,128]{2,1,0:T(8,128)} %squeeze.9.u_in, f32[32,32,128]{2,1,0:T(8,128)} %squeeze.10.f_in, f32[32,32,128]{2,1,0:T(8,128)} %squeeze.11.k_in, f32[26]{0:T(128)} %w_ref.1, f32[32]{0:T(128)} %om_ref.1), custom_call_target="tpu_custom_call" | custom-call | tf_op jit(solution)/shard_map/pallas_call | solution.py:214
  191.7 1.7 reshape.18
  193.4 0.1 copy.26
  193.5 0.9 copy.27
  194.5 0.7 reshape.22
  195.2 6.3 %all_to_all.34 = f32[2,1,65536]{2,1,0:T(1,128)S(1)} all-to-all(f32[2,1,65536]{2,1,0:T(1,128)S(1)} %reshape.22), channel_id=1, replica_groups=mesh['batch'=1,'gz'=4,'gy'=4,'gx'=2] {'gx'}, dimensions={0} | all-to-all | bytes 1048576 | tf_op jit(solution)/shard_map/all_to_all | solution.py:208
  201.4 2.3 %reduce.1 = f32[2,65536]{1,0:T(2,128)S(1)} reduce(f32[2,1,65536]{2,1,0:T(1,128)S(1)} %all_to_all.34, f32[]{:T(128)} %broadcast), dimensions={1}, to_apply=%all_to_all.27.reduce_sub_computation | reduce | bytes 1048580 | tf_op jit(solution)/shard_map/all_to_all | solution.py:208
  203.7 0.6 reshape.23
  204.4 1.1 copy.28

commit v2 on v1

v2 whole, which is shorter than its diff:
```python
import functools

import jax
import jax.numpy as jnp
from jax import lax
from jax.experimental import pallas as pl
from jax.experimental.pallas import tpu as pltpu
from jax.sharding import PartitionSpec as P

MESH = pl.DeviceIdType.MESH
F32 = jnp.float32
DEPTH = 4
ROW0 = 8
LANES = 128

OFFSETS = [(b, c, a) for a in (-1, 0, 1) for b in (-1, 0, 1) for c in (-1, 0, 1) if (a, b, c) != (0, 0, 0)]


def lane_of(shape):
    return lax.broadcasted_iota(jnp.int32, shape, len(shape) - 1)


def repeat(count, body):
    lax.fori_loop(0, count, lambda i, carry: (body(i), carry)[1], 0, unroll=count)


def shift_x(v, c, half):
    lane = lane_of(v.shape) % half
    if c == 1:
        return jnp.where(lane == half - 1, pltpu.roll(v, half - 1, v.ndim - 1), pltpu.roll(v, 2 * half - 1, v.ndim - 1))
    return jnp.where(lane == 0, pltpu.roll(v, half + 1, v.ndim - 1), pltpu.roll(v, 1, v.ndim - 1))


def kernel(dims, u_in, f_in, k_in, w_ref, om_ref, out_ref,
           ext, temp, coef, nat, zsend, zrecv, drecv,
           send_sem, recv_sem, here_sem, pair_send, pair_recv):
    n_y, n_z, ny, nz, sweeps, tiles = dims
    s = DEPTH
    half = LANES // 2
    lo, hi = ROW0, ROW0 + nz
    qe = ny + 2 * s
    first = lo - s + 1
    bx = u_in.shape[0]

    core = lax.axis_index("gx")
    gy = lax.axis_index("gy")
    gz = lax.axis_index("gz")
    zhi, zlo = lax.rem(gz + 1, n_z), lax.rem(gz + n_z - 1, n_z)
    other = 1 - core
    yhi = lax.rem(gy + core, n_y)
    ylo = lax.rem(gy + n_y - other, n_y)

    neighbours = [
        {"gx": other, "gy": yhi, "gz": zhi}, {"gx": other, "gy": ylo, "gz": zhi},
        {"gx": other, "gy": yhi, "gz": zlo}, {"gx": other, "gy": ylo, "gz": zlo},
        {"gz": zhi}, {"gz": zlo}, {"gx": other, "gy": yhi}, {"gx": other, "gy": ylo},
    ]

    barrier = pltpu.get_barrier_semaphore()
    for nb in neighbours:
        pl.semaphore_signal(barrier, inc=1, device_id=nb, device_id_type=MESH)

    mine = pl.multiple_of(core * ny, ny)
    theirs = pl.multiple_of(other * ny, ny)
    my_x = pl.ds(core * bx, bx)
    kap, frc = 2, 3
    fields = (u_in, k_in, f_in)
    kept = [pltpu.make_async_copy(src.at[:, pl.ds(mine, ny)], nat.at[i, my_x], here_sem.at[i])
            for i, src in enumerate(fields)]
    given = [pltpu.make_async_remote_copy(
        src_ref=src.at[:, pl.ds(theirs, ny)], dst_ref=nat.at[i, my_x], send_sem=pair_send.at[i],
        recv_sem=pair_recv.at[i], device_id={"gx": other}, device_id_type=MESH)
        for i, src in enumerate(fields)]
    for i in (1, 2, 0):
        kept[i].start()

    hq = ny // 2

    def copies(arr, slot):
        pieces = [
            (zsend.at[slot, 0, pl.ds((hq - s) * s, s * s)], drecv.at[slot, 0]),
            (zsend.at[slot, 0, pl.ds(0, s * s)], drecv.at[slot, 1]),
            (zsend.at[slot, 1, pl.ds((hq - s) * s, s * s)], drecv.at[slot, 2]),
            (zsend.at[slot, 1, pl.ds(0, s * s)], drecv.at[slot, 3]),
            (zsend.at[slot, 0], zrecv.at[slot, 0]),
            (zsend.at[slot, 1], zrecv.at[slot, 1]),
            (ext.at[arr, pl.ds(ny, s), pl.ds(lo, nz)], ext.at[arr, pl.ds(0, s), pl.ds(lo, nz)]),
            (ext.at[arr, pl.ds(s, s), pl.ds(lo, nz)], ext.at[arr, pl.ds(ny + s, s), pl.ds(lo, nz)]),
        ]
        return [
            pltpu.make_async_remote_copy(
                src_ref=src, dst_ref=dst, send_sem=send_sem.at[slot, i], recv_sem=recv_sem.at[slot, i],
                device_id=neighbours[i], device_id_type=MESH)
            for i, (src, dst) in enumerate(pieces)
        ]

    left = lane_of((s, LANES)) < half

    def swap(v):
        return pltpu.roll(v, half, 1)

    def begin(arr, slot):
        def pack(q):
            top = jnp.where(left, swap(ext[arr, s + q, pl.ds(hi - s, s)]), ext[arr, s + q + hq, pl.ds(hi - s, s)])
            zsend[slot, 0, pl.ds(q * s, s)] = top
            bottom = jnp.where(left, ext[arr, s + q, pl.ds(lo, s)], swap(ext[arr, s + q + hq, pl.ds(lo, s)]))
            zsend[slot, 1, pl.ds(q * s, s)] = bottom

        repeat(hq, pack)
        for cp in copies(arr, slot):
            cp.start()

    def finish(arr, slot):
        for cp in copies(arr, slot):
            cp.wait()
        def fill(q, low, high):
            ext[arr, q, pl.ds(lo - s, s)] = jnp.where(left, low, swap(ext[arr, q, pl.ds(hi - s, s)]))
            ext[arr, q, pl.ds(hi, s)] = jnp.where(left, swap(ext[arr, q, pl.ds(lo, s)]), high)

        def at(ref, i, q):
            return ref[slot, i, pl.ds(q * s, s)]

        repeat(s, lambda q: fill(q, swap(at(drecv, 0, q)), at(drecv, 2, q)))
        repeat(hq, lambda q: fill(s + q, at(zrecv, 0, q), swap(at(zrecv, 1, q))))
        repeat(hq, lambda q: fill(s + hq + q, swap(at(zrecv, 0, q)), at(zrecv, 1, q)))
        repeat(s, lambda q: fill(s + ny + q, at(drecv, 1, q), swap(at(drecv, 3, q))))

    pl.semaphore_wait(barrier, len(neighbours))
    for i in (1, 2, 0):
        given[i].start()

    @pl.loop(0, 3)
    def _(turn):
        i = lax.rem(turn + 1, 3)
        arr = i + lax.div(i + 1, 2)
        pltpu.make_async_copy(u_in.at[:, pl.ds(mine, ny)], nat.at[i, my_x], here_sem.at[i]).wait()
        pltpu.make_async_remote_copy(
            src_ref=u_in.at[:, pl.ds(theirs, ny)], dst_ref=nat.at[i, my_x], send_sem=pair_send.at[i],
            recv_sem=pair_recv.at[i], device_id={"gx": other}, device_id_type=MESH).wait()

        @pl.loop(0, ny // 8)
        def _(yt):
            y0 = pl.multiple_of(yt * 8, 8)
            planes = jnp.swapaxes(nat[i, :, pl.ds(y0, 8), :], 0, 1)
            for y in range(8):
                turned = planes[y].T
                ext[arr, s + y0 + y, pl.ds(lo, nz)] = jnp.concatenate([turned[:nz], turned[nz:]], axis=1)

        begin(arr, arr)

    @pl.loop(kap, frc + 1)
    def _(arr):
        finish(arr, arr)

    @pl.loop(1, qe - 1)
    def _(q):
        def tile(t):
            base = first + 8 * t
            k_ab = {(a, b): ext[kap, q + a, pl.ds(base + b, 8)] for a in (-1, 0, 1) for b in (-1, 0, 1)}
            k_mid = k_ab[0, 0]
            mids = {0: k_mid, 1: shift_x(k_mid, -1, half), -1: shift_x(k_mid, 1, half)}
            raw, sums = [], {}
            for m, (a, b, c) in enumerate(OFFSETS):
                d = (0.5 * w_ref[m]) * (mids[c] + k_ab[a, b])
                raw.append(d)
                sums[c] = d if c not in sums else sums[c] + d
            diag = sums[0] + shift_x(sums[1], 1, half) + shift_x(sums[-1], -1, half)
            inv = 1.0 / diag
            invs = {0: inv, 1: shift_x(inv, -1, half), -1: shift_x(inv, 1, half)}
            for m, (a, b, c) in enumerate(OFFSETS):
                coef[q - 1, t, m] = raw[m] * invs[c]
            coef[q - 1, t, len(OFFSETS)] = ext[frc, q, pl.ds(base, 8)] * inv

        repeat(tiles, tile)

    def update(src, dst, relax, q_lo, q_hi, which, unroll):
        def block(q0, n):
            for t in which:
                base = first + 8 * t
                rows = {b: src[pl.ds(q0 - 1, n + 2), pl.ds(base + b, 8)] for b in (-1, 0, 1)}
                sums = {0: coef[pl.ds(q0 - 1, n), t, len(OFFSETS)]}
                for m, (a, b, c) in enumerate(OFFSETS):
                    p = coef[pl.ds(q0 - 1, n), t, m] * rows[b][1 + a:1 + a + n]
                    sums[c] = p if c not in sums else sums[c] + p
                total = sums[0] + shift_x(sums[1], 1, half) + shift_x(sums[-1], -1, half)
                mid = rows[0][1:1 + n]
                dst[pl.ds(q0, n), pl.ds(base, 8)] = mid + relax * (total - mid)

        count = q_hi - q_lo
        if count // unroll == 1:
            block(q_lo, unroll)
        elif count >= unroll:
            @pl.loop(0, count // unroll)
            def _(blk):
                block(q_lo + blk * unroll, unroll)

        if count % unroll:
            block(q_lo + count // unroll * unroll, count % unroll)

    every = tuple(range(tiles))
    inner_first = tuple(t for t in every if first + 8 * t > lo and first + 8 * t + 8 < hi)
    outer_first = tuple(t for t in every if t not in inner_first)
    inner_last = tuple(t for t in every if first + 8 * t >= lo + s and first + 8 * t + 8 <= hi - s)
    outer_last = tuple(t for t in every if t not in inner_last)

    def group(slot, k0, send):
        arr, nxt = ext.at[slot], ext.at[1 - slot]
        relax = om_ref[k0]
        update(arr, temp, relax, s + 1, s + ny - 1, inner_first, 6)
        finish(slot, slot)
        update(arr, temp, relax, 1, s + 1, every, 4)
        update(arr, temp, relax, s + 1, s + ny - 1, outer_first, 6)
        update(arr, temp, relax, s + ny - 1, qe - 1, every, 4)
        bufs = [arr, temp]
        for j in range(1, s - 1):
            update(bufs[j % 2], bufs[(j + 1) % 2], om_ref[k0 + j], 1 + j, qe - 1 - j, every, 4)
        src, relax = bufs[(s - 1) % 2], om_ref[k0 + s - 1]
        update(src, nxt, relax, s, 2 * s, every, 4)
        update(src, nxt, relax, ny, ny + s, every, 4)
        update(src, nxt, relax, 2 * s, ny, outer_last, 4)
        send()
        update(src, nxt, relax, 2 * s, ny, inner_last, 6)

    groups = sweeps // s

    @pl.loop(0, groups)
    def _(i):
        slot = lax.rem(i, 2)

        def send():
            @pl.when(i < groups - 1)
            def _():
                begin(1 - slot, 1 - slot)

        group(slot, s * i, send)

    last = groups % 2

    def home(yt):
        rows = pl.ds(pl.multiple_of(core * ny + yt * 8, 8), 8)
        return (pltpu.make_async_copy(
                    nat.at[0, my_x, pl.ds(pl.multiple_of(yt * 8, 8), 8)], out_ref.at[:, rows], here_sem.at[yt]),
                pltpu.make_async_remote_copy(
                    src_ref=nat.at[0, pl.ds(other * bx, bx), pl.ds(pl.multiple_of(yt * 8, 8), 8)], dst_ref=out_ref.at[:, rows],
                    send_sem=pair_send.at[yt], recv_sem=pair_recv.at[yt], device_id={"gx": other},
                    device_id_type=MESH))

    @pl.loop(0, ny // 8)
    def _(step):
        yt = pl.multiple_of(step * 8, 8)
        planes = []
        for y in range(8):
            row = ext[last, s + yt + y, pl.ds(lo, nz)]
            planes.append(jnp.concatenate([row[:, :half], row[:, half:]], axis=0).T)
        nat[0, :, pl.ds(yt, 8), :] = jnp.swapaxes(jnp.stack(planes), 0, 1)
        for cp in home(step):
            cp.start()

    @pl.loop(0, ny // 8)
    def _(step):
        for cp in home(step):
            cp.wait()


def solution(mesh):
    spec = P(("batch", "gx"), "gy", "gz")
    n_x, n_y, n_z = mesh.shape["gx"], mesh.shape["gy"], mesh.shape["gz"]

    def local(u, f, k, w, om):
        bx, by, bz = u.shape
        ny, nz = by // n_x, bz // 2
        s = DEPTH
        tiles = -(-(nz + 2 * s - 2) // 8)
        rows = ROW0 + -(-(nz + s) // 8) * 8
        qe = ny + 2 * s
        hbm = pl.BlockSpec(memory_space=pl.ANY)
        sm = pl.BlockSpec(memory_space=pltpu.SMEM)
        dma = pltpu.SemaphoreType.DMA
        return pl.pallas_call(
            functools.partial(kernel, (n_y, n_z, ny, nz, om.shape[0], tiles)),
            out_shape=jax.ShapeDtypeStruct(u.shape, F32),
            in_specs=[hbm, hbm, hbm, sm, sm],
            out_specs=hbm,
            scratch_shapes=[
                pltpu.VMEM((4, qe, rows, LANES), F32),
                pltpu.VMEM((qe, rows, LANES), F32),
                pltpu.VMEM((qe - 2, tiles, len(OFFSETS) + 2, 8, LANES), F32),
                pltpu.VMEM((3, n_x * bx, ny, bz), F32),
                pltpu.VMEM((4, 2, ny // 2 * s, LANES), F32),
                pltpu.VMEM((4, 2, ny // 2 * s, LANES), F32),
                pltpu.VMEM((4, 4, s * s, LANES), F32),
                dma((4, 8)), dma((4, 8)), dma((4,)), dma((4,)), dma((4,)),
            ],
            compiler_params=pltpu.CompilerParams(collective_id=0, has_side_effects=True, vmem_limit_bytes=56 << 20),
        )(u, f, k, w, om)

    return jax.shard_map(local, mesh=mesh, in_specs=(spec, spec, spec, P(), P()), out_specs=spec, check_vma=False)
```

time: 206 us -> 108 us (0.52)
  local copies, waits for them, and re-layouts: 42.5 us -> 2.31 us
  Pallas kernels: 140 us -> 105 us
  blocking collectives: 13.9 us -> 0 us
  other arithmetic: 9.32 us -> 0 us
    pallas_call x1, Pallas kernels: 140 us -> 105 us  [local(): pl.pallas_call(functools.partial(kernel, (n_y, n_z, ny, nz, om.shape[0],...]
    all_to_all x2 -> x0, blocking collectives: 13.9 us -> none  [the longest x1 7.69 us: to_lanes(): v = lax.all_to_all(v, 'gx', 2, 1, tiled=True)]
    slice x4 -> x0, local copies, waits for them, and re-layouts: 11.4 us -> none  [the longest x2 7.37 us: local(): packed[2]]
    reshape x4 -> x0, local copies, waits for them, and re-layouts: 9.81 us -> none  [the longest x1 7.11 us: to_lanes(): v = v.reshape(3, bx * n_x, ny, 2, nz)]
    all_to_all x2 -> x0, other arithmetic: 8.96 us -> none  [the longest x1 6.64 us: to_lanes(): v = lax.all_to_all(v, 'gx', 2, 1, tiled=True)]
    unnamed x5 -> x1, local copies, waits for them, and re-layouts: 9.18 us -> 2.31 us
    all_to_all x3 -> x0, local copies, waits for them, and re-layouts: 5.14 us -> none  [the longest x2 4.07 us: to_lanes(): v = lax.all_to_all(v, 'gx', 2, 1, tiled=True)]
    squeeze x3 -> x0, local copies, waits for them, and re-layouts: 4.19 us -> none  [the longest x1 1.41 us: local(): packed[1]]
where the time goes in v2:
time: 108 us
  Pallas kernels  105 us (97%)
  local copies, waits for them, and re-layouts  2.31 us (2%)
    pallas_call x1, Pallas kernels, local(): pl.pallas_call(functools.partial(kernel, (n_y, n_z, ny, nz, om.shape[0],...  105 us
    unnamed x1, local copies, waits for them, and re-layouts  2.31 us

profile of v2, /device:TPU:97, one launch (start us, length us, event | category | flops | bytes accessed | tf_op | source)
XLA Modules:
  0.0 107.7 jit_solution(5993534999870986491)
XLA Ops:
  0.0 105.4 %shard_map.55 = f32[32,64,64]{2,1,0:T(8,128)} custom-call(f32[32,64,64]{2,1,0:T(8,128)} %u_in.1, f32[32,64,64]{2,1,0:T(8,128)} %f_in.1, f32[32,64,64]{2,1,0:T(8,128)} %k_in.1, f32[26]{0:T(128)} %w_ref.1, f32[32]{0:T(128)} %om_ref.1), custom_call_target="tpu_custom_call" | custom-call | tf_op jit(solution)/shard_map/pallas_call | solution.py:279
  105.4 2.3 %copy.7 = f32[32,64,64]{2,1,0:T(8,128)} copy(f32[32,64,64]{2,1,0:T(8,128)} %shard_map.55) | data formatting | bytes 1048576

commit v3 on v2

--- a/solution.py
+++ b/solution.py
@@ -12,6 +12,7 @@
 DEPTH = 4
 ROW0 = 8
 LANES = 128
+N0, N1, N2, N3 = 10, 6, 8, 8
 
 OFFSETS = [(b, c, a) for a in (-1, 0, 1) for b in (-1, 0, 1) for c in (-1, 0, 1) if (a, b, c) != (0, 0, 0)]
 
@@ -24,22 +25,23 @@
     lax.fori_loop(0, count, lambda i, carry: (body(i), carry)[1], 0, unroll=count)
 
 
-def shift_x(v, c, half):
-    lane = lane_of(v.shape) % half
-    if c == 1:
-        return jnp.where(lane == half - 1, pltpu.roll(v, half - 1, v.ndim - 1), pltpu.roll(v, 2 * half - 1, v.ndim - 1))
-    return jnp.where(lane == 0, pltpu.roll(v, half + 1, v.ndim - 1), pltpu.roll(v, 1, v.ndim - 1))
+def turn_lanes(v, by):
+    return pltpu.roll(v, -by % LANES, v.ndim - 1)
+
+
+def shift_x(v, c):
+    return turn_lanes(v, 2 * c)
 
 
 def kernel(dims, u_in, f_in, k_in, w_ref, om_ref, out_ref,
-           ext, temp, coef, nat, zsend, zrecv, drecv,
+           ext, temp, coef, nat, stage, zsend, zrecv, drecv,
            send_sem, recv_sem, here_sem, pair_send, pair_recv):
     n_y, n_z, ny, nz, sweeps, tiles = dims
     s = DEPTH
     half = LANES // 2
     lo, hi = ROW0, ROW0 + nz
     qe = ny + 2 * s
-    first = lo - s + 1
+    first = lo - s
     bx = u_in.shape[0]
 
     core = lax.axis_index("gx")
@@ -94,10 +96,10 @@
             for i, (src, dst) in enumerate(pieces)
         ]
 
-    left = lane_of((s, LANES)) < half
+    left = lane_of((s, LANES)) % 2 == 0
 
     def swap(v):
-        return pltpu.roll(v, half, 1)
+        return jnp.where(left, turn_lanes(v, 1), turn_lanes(v, -1))
 
     def begin(arr, slot):
         def pack(q):
@@ -143,38 +145,52 @@
             y0 = pl.multiple_of(yt * 8, 8)
             planes = jnp.swapaxes(nat[i, :, pl.ds(y0, 8), :], 0, 1)
             for y in range(8):
-                turned = planes[y].T
-                ext[arr, s + y0 + y, pl.ds(lo, nz)] = jnp.concatenate([turned[:nz], turned[nz:]], axis=1)
+                stage[y, pl.ds(0, half, stride=2), pl.ds(0, nz)] = planes[y][:, :nz]
+                stage[y, pl.ds(1, half, stride=2), pl.ds(0, nz)] = planes[y][:, nz:]
+                ext[arr, s + y0 + y, pl.ds(lo, nz)] = stage[y, :, pl.ds(0, nz)].T
 
         begin(arr, arr)
+
+    every = tuple(range(tiles))
+    inner = tuple(t for t in every if first + 8 * t > lo and first + 8 * t + 8 < hi)
+    outer = tuple(t for t in every if t not in inner)
+    half_w = [0.5 * w_ref[m] for m in range(len(OFFSETS))]
+    w_sum = functools.reduce(lambda x, y: x + y, half_w)
+
+    def coefficients(which, q_lo, n, trips, stride):
+        @pl.loop(0, trips)
+        def _(trip):
+            q0 = q_lo + trip * stride
+            for t in which:
+                base = first + 8 * t
+                rows = {b: ext[kap, pl.ds(q0 - 1, n + 2), pl.ds(base + b, 8)] for b in (-1, 0, 1)}
+                near = {(a, b): rows[b][1 + a:1 + a + n] for a in (-1, 0, 1) for b in (-1, 0, 1)}
+                mid = near[0, 0]
+                sums = {0: w_sum * mid}
+                for m, (a, b, c) in enumerate(OFFSETS):
+                    d = half_w[m] * near[a, b]
+                    sums[c] = d if c not in sums else sums[c] + d
+                inv = 1.0 / (sums[0] + shift_x(sums[1], 1) + shift_x(sums[-1], -1))
+                mids = {0: mid, 1: shift_x(mid, -1), -1: shift_x(mid, 1)}
+                invs = {0: inv, 1: shift_x(inv, -1), -1: shift_x(inv, 1)}
+                for m, (a, b, c) in enumerate(OFFSETS):
+                    coef[pl.ds(q0 - 1, n), t, m] = half_w[m] * (mids[c] + near[a, b]) * invs[c]
+                coef[pl.ds(q0 - 1, n), t, len(OFFSETS)] = ext[frc, pl.ds(q0, n), pl.ds(base, 8)] * inv
+
+    CN = 2
+    coefficients(inner, s + 1, CN, (ny - 2) // CN, CN)
 
     @pl.loop(kap, frc + 1)
     def _(arr):
         finish(arr, arr)
 
-    @pl.loop(1, qe - 1)
-    def _(q):
-        def tile(t):
-            base = first + 8 * t
-            k_ab = {(a, b): ext[kap, q + a, pl.ds(base + b, 8)] for a in (-1, 0, 1) for b in (-1, 0, 1)}
-            k_mid = k_ab[0, 0]
-            mids = {0: k_mid, 1: shift_x(k_mid, -1, half), -1: shift_x(k_mid, 1, half)}
-            raw, sums = [], {}
-            for m, (a, b, c) in enumerate(OFFSETS):
-                d = (0.5 * w_ref[m]) * (mids[c] + k_ab[a, b])
-                raw.append(d)
-                sums[c] = d if c not in sums else sums[c] + d
-            diag = sums[0] + shift_x(sums[1], 1, half) + shift_x(sums[-1], -1, half)
-            inv = 1.0 / diag
-            invs = {0: inv, 1: shift_x(inv, -1, half), -1: shift_x(inv, 1, half)}
-            for m, (a, b, c) in enumerate(OFFSETS):
-                coef[q - 1, t, m] = raw[m] * invs[c]
-            coef[q - 1, t, len(OFFSETS)] = ext[frc, q, pl.ds(base, 8)] * inv
-
-        repeat(tiles, tile)
-
-    def update(src, dst, relax, q_lo, q_hi, which, unroll):
-        def block(q0, n):
+    coefficients(outer, s + 1, CN, (ny - 2) // CN, CN)
+    coefficients(every, 1, s, 2, qe - 2 - s)
+
+    def update(src, dst, relax, which, q_lo, n, trips, stride=None):
+        @pl.loop(0, trips)
+        def _(trip):
+            q0 = q_lo + trip * (stride or n)
             for t in which:
                 base = first + 8 * t
                 rows = {b: src[pl.ds(q0 - 1, n + 2), pl.ds(base + b, 8)] for b in (-1, 0, 1)}
@@ -182,44 +198,26 @@
                 for m, (a, b, c) in enumerate(OFFSETS):
                     p = coef[pl.ds(q0 - 1, n), t, m] * rows[b][1 + a:1 + a + n]
                     sums[c] = p if c not in sums else sums[c] + p
-                total = sums[0] + shift_x(sums[1], 1, half) + shift_x(sums[-1], -1, half)
+                total = sums[0] + shift_x(sums[1], 1) + shift_x(sums[-1], -1)
                 mid = rows[0][1:1 + n]
                 dst[pl.ds(q0, n), pl.ds(base, 8)] = mid + relax * (total - mid)
 
-        count = q_hi - q_lo
-        if count // unroll == 1:
-            block(q_lo, unroll)
-        elif count >= unroll:
-            @pl.loop(0, count // unroll)
-            def _(blk):
-                block(q_lo + blk * unroll, unroll)
-
-        if count % unroll:
-            block(q_lo + count // unroll * unroll, count % unroll)
-
-    every = tuple(range(tiles))
-    inner_first = tuple(t for t in every if first + 8 * t > lo and first + 8 * t + 8 < hi)
-    outer_first = tuple(t for t in every if t not in inner_first)
-    inner_last = tuple(t for t in every if first + 8 * t >= lo + s and first + 8 * t + 8 <= hi - s)
-    outer_last = tuple(t for t in every if t not in inner_last)
-
     def group(slot, k0, send):
         arr, nxt = ext.at[slot], ext.at[1 - slot]
+        bufs = [arr, temp]
         relax = om_ref[k0]
-        update(arr, temp, relax, s + 1, s + ny - 1, inner_first, 6)
+        update(arr, temp, relax, inner, s + 1, N0, (ny - 2) // N0)
         finish(slot, slot)
-        update(arr, temp, relax, 1, s + 1, every, 4)
-        update(arr, temp, relax, s + 1, s + ny - 1, outer_first, 6)
-        update(arr, temp, relax, s + ny - 1, qe - 1, every, 4)
-        bufs = [arr, temp]
+        update(arr, temp, relax, outer, s + 1, N0, (ny - 2) // N0)
+        update(arr, temp, relax, every, 1, s, 2, qe - 2 - s)
         for j in range(1, s - 1):
-            update(bufs[j % 2], bufs[(j + 1) % 2], om_ref[k0 + j], 1 + j, qe - 1 - j, every, 4)
+            rows_now = qe - 2 - 2 * j
+            update(bufs[j % 2], bufs[(j + 1) % 2], om_ref[k0 + j], every, 1 + j, N1, -(-rows_now // N1))
         src, relax = bufs[(s - 1) % 2], om_ref[k0 + s - 1]
-        update(src, nxt, relax, s, 2 * s, every, 4)
-        update(src, nxt, relax, ny, ny + s, every, 4)
-        update(src, nxt, relax, 2 * s, ny, outer_last, 4)
+        update(src, nxt, relax, every, s, s, 2, ny - s)
+        update(src, nxt, relax, outer, 2 * s, N2, (ny - 2 * s) // N2)
         send()
-        update(src, nxt, relax, 2 * s, ny, inner_last, 6)
+        update(src, nxt, relax, inner, 2 * s, N3, (ny - 2 * s) // N3)
 
     groups = sweeps // s
 
@@ -250,8 +248,9 @@
         yt = pl.multiple_of(step * 8, 8)
         planes = []
         for y in range(8):
-            row = ext[last, s + yt + y, pl.ds(lo, nz)]
-            planes.append(jnp.concatenate([row[:, :half], row[:, half:]], axis=0).T)
+            stage[y, :, pl.ds(0, nz)] = ext[last, s + yt + y, pl.ds(lo, nz)].T
+            planes.append(jnp.concatenate([stage[y, pl.ds(0, half, stride=2), pl.ds(0, nz)],
+                                           stage[y, pl.ds(1, half, stride=2), pl.ds(0, nz)]], axis=1))
         nat[0, :, pl.ds(yt, 8), :] = jnp.swapaxes(jnp.stack(planes), 0, 1)
         for cp in home(step):
             cp.start()
@@ -270,7 +269,7 @@
         bx, by, bz = u.shape
         ny, nz = by // n_x, bz // 2
         s = DEPTH
-        tiles = -(-(nz + 2 * s - 2) // 8)
+        tiles = -(-(nz + 2 * s - 1) // 8)
         rows = ROW0 + -(-(nz + s) // 8) * 8
         qe = ny + 2 * s
         hbm = pl.BlockSpec(memory_space=pl.ANY)
@@ -286,6 +285,7 @@
                 pltpu.VMEM((qe, rows, LANES), F32),
                 pltpu.VMEM((qe - 2, tiles, len(OFFSETS) + 2, 8, LANES), F32),
                 pltpu.VMEM((3, n_x * bx, ny, bz), F32),
+                pltpu.VMEM((8, LANES, LANES), F32),
                 pltpu.VMEM((4, 2, ny // 2 * s, LANES), F32),
                 pltpu.VMEM((4, 2, ny // 2 * s, LANES), F32),
                 pltpu.VMEM((4, 4, s * s, LANES), F32),

time: 108 us -> 95.5 us (0.88)
  Pallas kernels: 105 us -> 93.1 us
    pallas_call x1, Pallas kernels: 105 us -> 93.1 us  [local(): pl.pallas_call(functools.partial(kernel, (n_y, n_z, ny, nz, om.shape[0],...]
where the time goes in v3:
time: 95.5 us; the launch traced here: 95.4 us
  Pallas kernels  93.1 us (97%)
  local copies, waits for them, and re-layouts  2.31 us (2%)
    pallas_call x1, Pallas kernels, local(): pl.pallas_call(functools.partial(kernel, (n_y, n_z, ny, nz, om.shape[0],...  93.1 us
    unnamed x1, local copies, waits for them, and re-layouts  2.31 us

profile of v3, /device:TPU:97, one launch (start us, length us, event | category | flops | bytes accessed | tf_op | source)
XLA Modules:
  0.0 95.4 jit_solution(11888862581502403362)
XLA Ops:
  0.0 93.1 %shard_map.55 = f32[32,64,64]{2,1,0:T(8,128)} custom-call(f32[32,64,64]{2,1,0:T(8,128)} %u_in.1, f32[32,64,64]{2,1,0:T(8,128)} %f_in.1, f32[32,64,64]{2,1,0:T(8,128)} %k_in.1, f32[26]{0:T(128)} %w_ref.1, f32[32]{0:T(128)} %om_ref.1), custom_call_target="tpu_custom_call" | custom-call | tf_op jit(solution)/shard_map/pallas_call | solution.py:278
  93.1 2.3 %copy.7 = f32[32,64,64]{2,1,0:T(8,128)} copy(f32[32,64,64]{2,1,0:T(8,128)} %shard_map.55) | data formatting | bytes 1048576

commit v4 on v3

--- a/solution.py
+++ b/solution.py
@@ -12,7 +12,7 @@
 DEPTH = 4
 ROW0 = 8
 LANES = 128
-N0, N1, N2, N3 = 10, 6, 8, 8
+N0, N1, N2, N3, N4 = 10, 12, 16, 12, 15
 
 OFFSETS = [(b, c, a) for a in (-1, 0, 1) for b in (-1, 0, 1) for c in (-1, 0, 1) if (a, b, c) != (0, 0, 0)]
 
@@ -34,7 +34,7 @@
 
 
 def kernel(dims, u_in, f_in, k_in, w_ref, om_ref, out_ref,
-           ext, temp, coef, nat, stage, zsend, zrecv, drecv,
+           ext, temp, coef, nat, stage, zsend, zrecv, dsend, drecv,
            send_sem, recv_sem, here_sem, pair_send, pair_recv):
     n_y, n_z, ny, nz, sweeps, tiles = dims
     s = DEPTH
@@ -78,12 +78,8 @@
 
     hq = ny // 2
 
-    def copies(arr, slot):
-        pieces = [
-            (zsend.at[slot, 0, pl.ds((hq - s) * s, s * s)], drecv.at[slot, 0]),
-            (zsend.at[slot, 0, pl.ds(0, s * s)], drecv.at[slot, 1]),
-            (zsend.at[slot, 1, pl.ds((hq - s) * s, s * s)], drecv.at[slot, 2]),
-            (zsend.at[slot, 1, pl.ds(0, s * s)], drecv.at[slot, 3]),
+    def copies(arr, slot, which):
+        pieces = [(dsend.at[slot, i], drecv.at[slot, i]) for i in range(4)] + [
             (zsend.at[slot, 0], zrecv.at[slot, 0]),
             (zsend.at[slot, 1], zrecv.at[slot, 1]),
             (ext.at[arr, pl.ds(ny, s), pl.ds(lo, nz)], ext.at[arr, pl.ds(0, s), pl.ds(lo, nz)]),
@@ -91,41 +87,72 @@
         ]
         return [
             pltpu.make_async_remote_copy(
-                src_ref=src, dst_ref=dst, send_sem=send_sem.at[slot, i], recv_sem=recv_sem.at[slot, i],
-                device_id=neighbours[i], device_id_type=MESH)
-            for i, (src, dst) in enumerate(pieces)
+                src_ref=pieces[i][0], dst_ref=pieces[i][1], send_sem=send_sem.at[slot, i],
+                recv_sem=recv_sem.at[slot, i], device_id=neighbours[i], device_id_type=MESH)
+            for i in which
         ]
 
+    CORNERS, Z_FACES, Y_FACES = (0, 1, 2, 3), (4, 5), (6, 7)
     left = lane_of((s, LANES)) % 2 == 0
+    below, bottom, top, above = (pl.ds(row, s) for row in (lo - s, lo, hi - s, hi))
 
     def swap(v):
         return jnp.where(left, turn_lanes(v, 1), turn_lanes(v, -1))
 
-    def begin(arr, slot):
+    def part(q):
+        return pl.ds(q * s, s)
+
+    def begin_z(arr, slot):
+        def corner(q):
+            for i, (q0, rows) in enumerate(((ny, top), (s, top), (ny, bottom), (s, bottom))):
+                dsend[slot, i, part(q)] = swap(ext[arr, q0 + q, rows])
+
         def pack(q):
-            top = jnp.where(left, swap(ext[arr, s + q, pl.ds(hi - s, s)]), ext[arr, s + q + hq, pl.ds(hi - s, s)])
-            zsend[slot, 0, pl.ds(q * s, s)] = top
-            bottom = jnp.where(left, ext[arr, s + q, pl.ds(lo, s)], swap(ext[arr, s + q + hq, pl.ds(lo, s)]))
-            zsend[slot, 1, pl.ds(q * s, s)] = bottom
+            zsend[slot, 0, part(q)] = jnp.where(
+                left, swap(ext[arr, s + q, top]), ext[arr, s + q + hq, top])
+            zsend[slot, 1, part(q)] = jnp.where(
+                left, ext[arr, s + q, bottom], swap(ext[arr, s + q + hq, bottom]))
 
         repeat(hq, pack)
-        for cp in copies(arr, slot):
+        for cp in copies(arr, slot, Z_FACES):
             cp.start()
-
-    def finish(arr, slot):
-        for cp in copies(arr, slot):
+        repeat(s, corner)
+        for cp in copies(arr, slot, CORNERS):
+            cp.start()
+
+    def begin_y(arr, slot):
+        for cp in copies(arr, slot, Y_FACES):
+            cp.start()
+
+        def local(q):
+            ext[arr, s + q, below] = swap(ext[arr, s + q, top])
+            ext[arr, s + q, above] = swap(ext[arr, s + q, bottom])
+
+        repeat(ny, local)
+
+    def finish_z(arr, slot):
+        for cp in copies(arr, slot, Z_FACES):
             cp.wait()
-        def fill(q, low, high):
-            ext[arr, q, pl.ds(lo - s, s)] = jnp.where(left, low, swap(ext[arr, q, pl.ds(hi - s, s)]))
-            ext[arr, q, pl.ds(hi, s)] = jnp.where(left, swap(ext[arr, q, pl.ds(lo, s)]), high)
-
-        def at(ref, i, q):
-            return ref[slot, i, pl.ds(q * s, s)]
-
-        repeat(s, lambda q: fill(q, swap(at(drecv, 0, q)), at(drecv, 2, q)))
-        repeat(hq, lambda q: fill(s + q, at(zrecv, 0, q), swap(at(zrecv, 1, q))))
-        repeat(hq, lambda q: fill(s + hq + q, swap(at(zrecv, 0, q)), at(zrecv, 1, q)))
-        repeat(s, lambda q: fill(s + ny + q, at(drecv, 1, q), swap(at(drecv, 3, q))))
+
+        def fill(q):
+            low, high = zrecv[slot, 0, part(q)], zrecv[slot, 1, part(q)]
+            ext[arr, s + q, below] = jnp.where(left, low, ext[arr, s + q, below])
+            ext[arr, s + q, above] = jnp.where(left, ext[arr, s + q, above], swap(high))
+            ext[arr, s + q + hq, below] = jnp.where(left, swap(low), ext[arr, s + q + hq, below])
+            ext[arr, s + q + hq, above] = jnp.where(left, ext[arr, s + q + hq, above], high)
+
+        repeat(hq, fill)
+
+    def finish_y(arr, slot):
+        for cp in copies(arr, slot, CORNERS + Y_FACES):
+            cp.wait()
+
+        def fill(q):
+            for i, q0 in ((0, 0), (1, s + ny)):
+                ext[arr, q0 + q, below] = jnp.where(left, drecv[slot, i, part(q)], swap(ext[arr, q0 + q, top]))
+                ext[arr, q0 + q, above] = jnp.where(left, swap(ext[arr, q0 + q, bottom]), drecv[slot, i + 2, part(q)])
+
+        repeat(s, fill)
 
     pl.semaphore_wait(barrier, len(neighbours))
     for i in (1, 2, 0):
@@ -149,7 +176,8 @@
                 stage[y, pl.ds(1, half, stride=2), pl.ds(0, nz)] = planes[y][:, nz:]
                 ext[arr, s + y0 + y, pl.ds(lo, nz)] = stage[y, :, pl.ds(0, nz)].T
 
-        begin(arr, arr)
+        begin_z(arr, arr)
+        begin_y(arr, arr)
 
     every = tuple(range(tiles))
     inner = tuple(t for t in every if first + 8 * t > lo and first + 8 * t + 8 < hi)
@@ -177,12 +205,13 @@
                     coef[pl.ds(q0 - 1, n), t, m] = half_w[m] * (mids[c] + near[a, b]) * invs[c]
                 coef[pl.ds(q0 - 1, n), t, len(OFFSETS)] = ext[frc, pl.ds(q0, n), pl.ds(base, 8)] * inv
 
-    CN = 2
+    CN = 5
     coefficients(inner, s + 1, CN, (ny - 2) // CN, CN)
 
     @pl.loop(kap, frc + 1)
     def _(arr):
-        finish(arr, arr)
+        finish_z(arr, arr)
+        finish_y(arr, arr)
 
     coefficients(outer, s + 1, CN, (ny - 2) // CN, CN)
     coefficients(every, 1, s, 2, qe - 2 - s)
@@ -202,35 +231,36 @@
                 mid = rows[0][1:1 + n]
                 dst[pl.ds(q0, n), pl.ds(base, 8)] = mid + relax * (total - mid)
 
-    def group(slot, k0, send):
+    groups = sweeps // s
+
+    @pl.loop(0, groups)
+    def _(i):
+        slot = lax.rem(i, 2)
         arr, nxt = ext.at[slot], ext.at[1 - slot]
         bufs = [arr, temp]
-        relax = om_ref[k0]
+        relax = om_ref[s * i]
         update(arr, temp, relax, inner, s + 1, N0, (ny - 2) // N0)
-        finish(slot, slot)
-        update(arr, temp, relax, outer, s + 1, N0, (ny - 2) // N0)
+        finish_z(slot, slot)
+        update(arr, temp, relax, outer, s + 1, N4, (ny - 2) // N4)
+        finish_y(slot, slot)
         update(arr, temp, relax, every, 1, s, 2, qe - 2 - s)
         for j in range(1, s - 1):
             rows_now = qe - 2 - 2 * j
-            update(bufs[j % 2], bufs[(j + 1) % 2], om_ref[k0 + j], every, 1 + j, N1, -(-rows_now // N1))
-        src, relax = bufs[(s - 1) % 2], om_ref[k0 + s - 1]
-        update(src, nxt, relax, every, s, s, 2, ny - s)
-        update(src, nxt, relax, outer, 2 * s, N2, (ny - 2 * s) // N2)
-        send()
+            update(bufs[j % 2], bufs[(j + 1) % 2], om_ref[s * i + j], every, 1 + j, N1, -(-rows_now // N1))
+        src, relax = bufs[(s - 1) % 2], om_ref[s * i + s - 1]
+        update(src, nxt, relax, outer, s, N2, ny // N2)
+
+        @pl.when(i < groups - 1)
+        def _():
+            begin_z(1 - slot, 1 - slot)
+
+        update(src, nxt, relax, inner, s, s, 2, ny - s)
+
+        @pl.when(i < groups - 1)
+        def _():
+            begin_y(1 - slot, 1 - slot)
+
         update(src, nxt, relax, inner, 2 * s, N3, (ny - 2 * s) // N3)
-
-    groups = sweeps // s
-
-    @pl.loop(0, groups)
-    def _(i):
-        slot = lax.rem(i, 2)
-
-        def send():
-            @pl.when(i < groups - 1)
-            def _():
-                begin(1 - slot, 1 - slot)
-
-        group(slot, s * i, send)
 
     last = groups % 2
 
@@ -289,6 +319,7 @@
                 pltpu.VMEM((4, 2, ny // 2 * s, LANES), F32),
                 pltpu.VMEM((4, 2, ny // 2 * s, LANES), F32),
                 pltpu.VMEM((4, 4, s * s, LANES), F32),
+                pltpu.VMEM((4, 4, s * s, LANES), F32),
                 dma((4, 8)), dma((4, 8)), dma((4,)), dma((4,)), dma((4,)),
             ],
             compiler_params=pltpu.CompilerParams(collective_id=0, has_side_effects=True, vmem_limit_bytes=56 << 20),

time: 95.5 us -> 88.9 us (0.931)
  Pallas kernels: 93.1 us -> 86.5 us
    pallas_call x1, Pallas kernels: 93.1 us -> 86.5 us  [local(): pl.pallas_call(functools.partial(kernel, (n_y, n_z, ny, nz, om.shape[0],...]
where the time goes in v4:
time: 88.9 us; the launch traced here: 88.8 us
  Pallas kernels  86.5 us (97%)
  local copies, waits for them, and re-layouts  2.31 us (3%)
    pallas_call x1, Pallas kernels, local(): pl.pallas_call(functools.partial(kernel, (n_y, n_z, ny, nz, om.shape[0],...  86.5 us
    unnamed x1, local copies, waits for them, and re-layouts  2.31 us

profile of v4, /device:TPU:97, one launch (start us, length us, event | category | flops | bytes accessed | tf_op | source)
XLA Modules:
  0.0 88.8 jit_solution(10012581705058099919)
XLA Ops:
  0.0 86.5 %shard_map.55 = f32[32,64,64]{2,1,0:T(8,128)} custom-call(f32[32,64,64]{2,1,0:T(8,128)} %u_in.1, f32[32,64,64]{2,1,0:T(8,128)} %f_in.1, f32[32,64,64]{2,1,0:T(8,128)} %k_in.1, f32[26]{0:T(128)} %w_ref.1, f32[32]{0:T(128)} %om_ref.1), custom_call_target="tpu_custom_call" | custom-call | tf_op jit(solution)/shard_map/pallas_call | solution.py:308
  86.5 2.3 %copy.7 = f32[32,64,64]{2,1,0:T(8,128)} copy(f32[32,64,64]{2,1,0:T(8,128)} %shard_map.55) | data formatting | bytes 1048576

commit v5 on v4

--- a/solution.py
+++ b/solution.py
@@ -12,7 +12,7 @@
 DEPTH = 4
 ROW0 = 8
 LANES = 128
-N0, N1, N2, N3, N4 = 10, 12, 16, 12, 15
+N0, N1, N2, N3, N4 = 10, 18, 16, 24, 30
 
 OFFSETS = [(b, c, a) for a in (-1, 0, 1) for b in (-1, 0, 1) for c in (-1, 0, 1) if (a, b, c) != (0, 0, 0)]
 
@@ -33,9 +33,9 @@
     return turn_lanes(v, 2 * c)
 
 
-def kernel(dims, u_in, f_in, k_in, w_ref, om_ref, out_ref,
+def kernel(dims, u_in, f_in, k_in, w_in, om_in, out_ref,
            ext, temp, coef, nat, stage, zsend, zrecv, dsend, drecv,
-           send_sem, recv_sem, here_sem, pair_send, pair_recv):
+           send_sem, recv_sem, here_sem, pair_send, pair_recv, w_ref, om_ref, scalar_sem):
     n_y, n_z, ny, nz, sweeps, tiles = dims
     s = DEPTH
     half = LANES // 2
@@ -69,12 +69,18 @@
     fields = (u_in, k_in, f_in)
     kept = [pltpu.make_async_copy(src.at[:, pl.ds(mine, ny)], nat.at[i, my_x], here_sem.at[i])
             for i, src in enumerate(fields)]
-    given = [pltpu.make_async_remote_copy(
-        src_ref=src.at[:, pl.ds(theirs, ny)], dst_ref=nat.at[i, my_x], send_sem=pair_send.at[i],
-        recv_sem=pair_recv.at[i], device_id={"gx": other}, device_id_type=MESH)
-        for i, src in enumerate(fields)]
+
+    def give(i, yt):
+        return pltpu.make_async_remote_copy(
+            src_ref=fields[i].at[:, pl.ds(pl.multiple_of(theirs + yt * 8, 8), 8)],
+            dst_ref=nat.at[i, my_x, pl.ds(pl.multiple_of(yt * 8, 8), 8)], send_sem=pair_send.at[i, yt],
+            recv_sem=pair_recv.at[i, yt], device_id={"gx": other}, device_id_type=MESH)
+
     for i in (1, 2, 0):
         kept[i].start()
+    scalars = [pltpu.make_async_copy(w_in, w_ref, scalar_sem.at[0]), pltpu.make_async_copy(om_in, om_ref, scalar_sem.at[1])]
+    for cp in scalars:
+        cp.start()
 
     hq = ny // 2
 
@@ -156,19 +162,20 @@
 
     pl.semaphore_wait(barrier, len(neighbours))
     for i in (1, 2, 0):
-        given[i].start()
+        for yt in range(ny // 8):
+            give(i, yt).start()
 
     @pl.loop(0, 3)
     def _(turn):
         i = lax.rem(turn + 1, 3)
         arr = i + lax.div(i + 1, 2)
         pltpu.make_async_copy(u_in.at[:, pl.ds(mine, ny)], nat.at[i, my_x], here_sem.at[i]).wait()
-        pltpu.make_async_remote_copy(
-            src_ref=u_in.at[:, pl.ds(theirs, ny)], dst_ref=nat.at[i, my_x], send_sem=pair_send.at[i],
-            recv_sem=pair_recv.at[i], device_id={"gx": other}, device_id_type=MESH).wait()
-
         @pl.loop(0, ny // 8)
         def _(yt):
+            pltpu.make_async_remote_copy(
+                src_ref=u_in.at[:, pl.ds(0, 8)], dst_ref=nat.at[i, my_x, pl.ds(pl.multiple_of(yt * 8, 8), 8)],
+                send_sem=pair_send.at[i, yt], recv_sem=pair_recv.at[i, yt], device_id={"gx": other},
+                device_id_type=MESH).wait()
             y0 = pl.multiple_of(yt * 8, 8)
             planes = jnp.swapaxes(nat[i, :, pl.ds(y0, 8), :], 0, 1)
             for y in range(8):
@@ -182,6 +189,8 @@
     every = tuple(range(tiles))
     inner = tuple(t for t in every if first + 8 * t > lo and first + 8 * t + 8 < hi)
     outer = tuple(t for t in every if t not in inner)
+    for cp in scalars:
+        cp.wait()
     half_w = [0.5 * w_ref[m] for m in range(len(OFFSETS))]
     w_sum = functools.reduce(lambda x, y: x + y, half_w)
 
@@ -205,16 +214,8 @@
                     coef[pl.ds(q0 - 1, n), t, m] = half_w[m] * (mids[c] + near[a, b]) * invs[c]
                 coef[pl.ds(q0 - 1, n), t, len(OFFSETS)] = ext[frc, pl.ds(q0, n), pl.ds(base, 8)] * inv
 
-    CN = 5
+    CN = 6
     coefficients(inner, s + 1, CN, (ny - 2) // CN, CN)
-
-    @pl.loop(kap, frc + 1)
-    def _(arr):
-        finish_z(arr, arr)
-        finish_y(arr, arr)
-
-    coefficients(outer, s + 1, CN, (ny - 2) // CN, CN)
-    coefficients(every, 1, s, 2, qe - 2 - s)
 
     def update(src, dst, relax, which, q_lo, n, trips, stride=None):
         @pl.loop(0, trips)
@@ -240,6 +241,17 @@
         bufs = [arr, temp]
         relax = om_ref[s * i]
         update(arr, temp, relax, inner, s + 1, N0, (ny - 2) // N0)
+
+        @pl.when(i == 0)
+        def _():
+            @pl.loop(kap, frc + 1)
+            def _(field):
+                finish_z(field, field)
+                finish_y(field, field)
+
+            coefficients(outer, s + 1, CN, (ny - 2) // CN, CN)
+            coefficients(every, 1, s, 2, qe - 2 - s)
+
         finish_z(slot, slot)
         update(arr, temp, relax, outer, s + 1, N4, (ny - 2) // N4)
         finish_y(slot, slot)
@@ -270,7 +282,7 @@
                     nat.at[0, my_x, pl.ds(pl.multiple_of(yt * 8, 8), 8)], out_ref.at[:, rows], here_sem.at[yt]),
                 pltpu.make_async_remote_copy(
                     src_ref=nat.at[0, pl.ds(other * bx, bx), pl.ds(pl.multiple_of(yt * 8, 8), 8)], dst_ref=out_ref.at[:, rows],
-                    send_sem=pair_send.at[yt], recv_sem=pair_recv.at[yt], device_id={"gx": other},
+                    send_sem=pair_send.at[0, yt], recv_sem=pair_recv.at[0, yt], device_id={"gx": other},
                     device_id_type=MESH))
 
     @pl.loop(0, ny // 8)
@@ -303,12 +315,11 @@
         rows = ROW0 + -(-(nz + s) // 8) * 8
         qe = ny + 2 * s
         hbm = pl.BlockSpec(memory_space=pl.ANY)
-        sm = pl.BlockSpec(memory_space=pltpu.SMEM)
         dma = pltpu.SemaphoreType.DMA
         return pl.pallas_call(
             functools.partial(kernel, (n_y, n_z, ny, nz, om.shape[0], tiles)),
             out_shape=jax.ShapeDtypeStruct(u.shape, F32),
-            in_specs=[hbm, hbm, hbm, sm, sm],
+            in_specs=[hbm, hbm, hbm, hbm, hbm],
             out_specs=hbm,
             scratch_shapes=[
                 pltpu.VMEM((4, qe, rows, LANES), F32),
@@ -320,7 +331,8 @@
                 pltpu.VMEM((4, 2, ny // 2 * s, LANES), F32),
                 pltpu.VMEM((4, 4, s * s, LANES), F32),
                 pltpu.VMEM((4, 4, s * s, LANES), F32),
-                dma((4, 8)), dma((4, 8)), dma((4,)), dma((4,)), dma((4,)),
+                dma((4, 8)), dma((4, 8)), dma((4,)), dma((3, ny // 8)), dma((3, ny // 8)),
+                pltpu.SMEM(w.shape, F32), pltpu.SMEM(om.shape, F32), dma((2,)),
             ],
             compiler_params=pltpu.CompilerParams(collective_id=0, has_side_effects=True, vmem_limit_bytes=56 << 20),
         )(u, f, k, w, om)

time: 88.9 us -> 86.1 us (0.969)
  Pallas kernels: 86.5 us -> 83.7 us
    pallas_call x1, Pallas kernels: 86.5 us -> 83.7 us  [local(): pl.pallas_call(functools.partial(kernel, (n_y, n_z, ny, nz, om.shape[0],...]
where the time goes in v5:
time: 86.1 us; the launch traced here: 86 us
  Pallas kernels  83.7 us (97%)
  local copies, waits for them, and re-layouts  2.31 us (3%)
    pallas_call x1, Pallas kernels, local(): pl.pallas_call(functools.partial(kernel, (n_y, n_z, ny, nz, om.shape[0],...  83.7 us
    unnamed x1, local copies, waits for them, and re-layouts  2.31 us

profile of v5, /device:TPU:97, one launch (start us, length us, event | category | flops | bytes accessed | tf_op | source)
XLA Modules:
  0.0 86.0 jit_solution(4530987656581641268)
XLA Ops:
  0.0 83.7 %shard_map.55 = f32[32,64,64]{2,1,0:T(8,128)} custom-call(f32[32,64,64]{2,1,0:T(8,128)} %u_in.1, f32[32,64,64]{2,1,0:T(8,128)} %f_in.1, f32[32,64,64]{2,1,0:T(8,128)} %k_in.1, f32[26]{0:T(128)} %w_in.1, f32[32]{0:T(128)} %om_in.1), custom_call_target="tpu_custom_call" | custom-call | tf_op jit(solution)/shard_map/pallas_call | solution.py:319
  83.7 2.3 %copy.7 = f32[32,64,64]{2,1,0:T(8,128)} copy(f32[32,64,64]{2,1,0:T(8,128)} %shard_map.55) | data formatting | bytes 1048576

commit v6 on v5

--- a/solution.py
+++ b/solution.py
@@ -108,16 +108,25 @@
     def part(q):
         return pl.ds(q * s, s)
 
+    low_rows = lax.broadcasted_iota(jnp.int32, (8, LANES), 0) < s
+    left_tile = lane_of((8, LANES)) % 2 == 0
+
     def begin_z(arr, slot):
+        def pack(q):
+            pairs = []
+            for row in (s + q, s + q + hq):
+                ends = jnp.where(low_rows, ext[arr, row, pl.ds(lo, 8)], ext[arr, row, pl.ds(hi - 8, 8)])
+                swapped = jnp.where(left_tile, turn_lanes(ends, 1), turn_lanes(ends, -1))
+                ext[arr, row, below] = swapped[s:]
+                ext[arr, row, above] = swapped[:s]
+                pairs.append((ends, swapped))
+            (ends_0, swapped_0), (ends_1, swapped_1) = pairs
+            zsend[slot, 0, part(q)] = jnp.where(left, swapped_0[s:], ends_1[s:])
+            zsend[slot, 1, part(q)] = jnp.where(left, ends_0[:s], swapped_1[:s])
+
         def corner(q):
-            for i, (q0, rows) in enumerate(((ny, top), (s, top), (ny, bottom), (s, bottom))):
-                dsend[slot, i, part(q)] = swap(ext[arr, q0 + q, rows])
-
-        def pack(q):
-            zsend[slot, 0, part(q)] = jnp.where(
-                left, swap(ext[arr, s + q, top]), ext[arr, s + q + hq, top])
-            zsend[slot, 1, part(q)] = jnp.where(
-                left, ext[arr, s + q, bottom], swap(ext[arr, s + q + hq, bottom]))
+            for i, (q0, rows) in enumerate(((ny, below), (s, below), (ny, above), (s, above))):
+                dsend[slot, i, part(q)] = ext[arr, q0 + q, rows]
 
         repeat(hq, pack)
         for cp in copies(arr, slot, Z_FACES):
@@ -129,12 +138,6 @@
     def begin_y(arr, slot):
         for cp in copies(arr, slot, Y_FACES):
             cp.start()
-
-        def local(q):
-            ext[arr, s + q, below] = swap(ext[arr, s + q, top])
-            ext[arr, s + q, above] = swap(ext[arr, s + q, bottom])
-
-        repeat(ny, local)
 
     def finish_z(arr, slot):
         for cp in copies(arr, slot, Z_FACES):

time: 86.1 us -> 85.5 us (level)
  no operation moved by 1% of the time
where the time goes in v6:
time: 85.5 us; the launch traced here: 85.3 us
  Pallas kernels  83 us (97%)
  local copies, waits for them, and re-layouts  2.31 us (3%)
    pallas_call x1, Pallas kernels, local(): pl.pallas_call(functools.partial(kernel, (n_y, n_z, ny, nz, om.shape[0],...  83 us
    unnamed x1, local copies, waits for them, and re-layouts  2.31 us

profile of v6, /device:TPU:97, one launch (start us, length us, event | category | flops | bytes accessed | tf_op | source)
XLA Modules:
  0.0 85.3 jit_solution(7921421590702456783)
XLA Ops:
  0.0 83.0 %shard_map.55 = f32[32,64,64]{2,1,0:T(8,128)} custom-call(f32[32,64,64]{2,1,0:T(8,128)} %u_in.1, f32[32,64,64]{2,1,0:T(8,128)} %f_in.1, f32[32,64,64]{2,1,0:T(8,128)} %k_in.1, f32[26]{0:T(128)} %w_in.1, f32[32]{0:T(128)} %om_in.1), custom_call_target="tpu_custom_call" | custom-call | tf_op jit(solution)/shard_map/pallas_call | solution.py:322
  83.0 2.3 %copy.7 = f32[32,64,64]{2,1,0:T(8,128)} copy(f32[32,64,64]{2,1,0:T(8,128)} %shard_map.55) | data formatting | bytes 1048576

commit v7 on v6

--- a/solution.py
+++ b/solution.py
@@ -12,7 +12,7 @@
 DEPTH = 4
 ROW0 = 8
 LANES = 128
-N0, N1, N2, N3, N4 = 10, 18, 16, 24, 30
+N0, N1, N2, N3, N4 = 30, 18, 16, 24, 30
 
 OFFSETS = [(b, c, a) for a in (-1, 0, 1) for b in (-1, 0, 1) for c in (-1, 0, 1) if (a, b, c) != (0, 0, 0)]
 
@@ -217,7 +217,7 @@
                     coef[pl.ds(q0 - 1, n), t, m] = half_w[m] * (mids[c] + near[a, b]) * invs[c]
                 coef[pl.ds(q0 - 1, n), t, len(OFFSETS)] = ext[frc, pl.ds(q0, n), pl.ds(base, 8)] * inv
 
-    CN = 6
+    CN = 10
     coefficients(inner, s + 1, CN, (ny - 2) // CN, CN)
 
     def update(src, dst, relax, which, q_lo, n, trips, stride=None):

time: 85.5 us -> 85.4 us (level)
  no operation moved by 1% of the time
where the time goes in v7:
time: 85.4 us; the launch traced here: 85.3 us
  Pallas kernels  83 us (97%)
  local copies, waits for them, and re-layouts  2.31 us (3%)
    pallas_call x1, Pallas kernels, local(): pl.pallas_call(functools.partial(kernel, (n_y, n_z, ny, nz, om.shape[0],...  83 us
    unnamed x1, local copies, waits for them, and re-layouts  2.31 us

profile of v7, /device:TPU:97, one launch (start us, length us, event | category | flops | bytes accessed | tf_op | source)
XLA Modules:
  0.0 85.3 jit_solution(16323825119002216285)
XLA Ops:
  0.0 83.0 %shard_map.55 = f32[32,64,64]{2,1,0:T(8,128)} custom-call(f32[32,64,64]{2,1,0:T(8,128)} %u_in.1, f32[32,64,64]{2,1,0:T(8,128)} %f_in.1, f32[32,64,64]{2,1,0:T(8,128)} %k_in.1, f32[26]{0:T(128)} %w_in.1, f32[32]{0:T(128)} %om_in.1), custom_call_target="tpu_custom_call" | custom-call | tf_op jit(solution)/shard_map/pallas_call | solution.py:322
  83.0 2.3 %copy.7 = f32[32,64,64]{2,1,0:T(8,128)} copy(f32[32,64,64]{2,1,0:T(8,128)} %shard_map.55) | data formatting | bytes 1048576
